TPU v7x, 32 devices: a whole 2x2x4 slice. The times are simulated.
32 devices in a mesh: grp: 2 (over core), dev: 16 (over z, y, x).
Axes of the slice: x: 2, y: 2, z: 4, core: 2. Of those that a mesh axis runs over, the one named last changes fastest.
Arguments:
- pixel_tiles: float32 [2048, 6, 512], P(('grp', 'dev')), may hold values from -31 to 31
- blend_source: int32 [2048, 2], P(('grp', 'dev')), may hold values from 0 to 15, all different within a row; in each aligned block of 64 rows (0 to 63, 64 to 127, ...) at most 8 rows name the same one
- blend_slot: int32 [2048, 2], P(('grp', 'dev')), may hold values from 0 to 63
- component_count: int32 [2048], P(('grp', 'dev')), may hold values from 12 to 24
- sed_start: bfloat16 [2048, 24, 6], P(('grp', 'dev')), may hold values from 0.049804688 to 0.5
- morph_start: bfloat16 [2048, 2, 24, 512], P(('grp', 'dev')), may hold values from 0.019897461 to 0.5
Outputs:
- whitened: float32 [2048, 6, 512], P(('grp', 'dev'))
- sed_final: bfloat16 [2048, 24, 6], P(('grp', 'dev'))
Inputs may be any that keep to these rules, and one draw needn't show every extreme that they name: `blend_source`: each blend names 2 different devices of its region; over the blends of one device no device is named more than 8 times, and some device is named exactly 8 times. `blend_slot`: several blends may name the same tile.
All inputs are finite; a program needn't handle non-finite values.
Results may differ from a plain program's by a relative error of at most 0.0052.
Values may be sent and summed in bfloat16 or wider, within the bound.
No kernel may reach another device: no remote copies, remote signals or barrier semaphores. Data moves between devices by JAX's collectives and lax.ppermute only.
A program may use at most 64 MiB of HBM per device.

v0:
```python
import math

import jax
import jax.numpy as jnp
from jax import lax
from jax.sharding import PartitionSpec as P

ITERS = 2


def fit_block(blend_data, sed, morph, count):
    components = sed.shape[1]
    active = (jnp.arange(components, dtype=jnp.int32)[None, :] < count[:, None]).astype(jnp.float32)
    sed = (sed.astype(jnp.float32) * active[:, :, None]).astype(jnp.bfloat16)
    morph = morph * active[:, None, :, None].astype(jnp.bfloat16)
    target = blend_data.astype(jnp.float32)
    for sweep in range(ITERS):
        model = jnp.einsum("nkb,nfkp->nfbp", sed, morph, preferred_element_type=jnp.float32)
        misfit = (model - target).astype(jnp.bfloat16)
        gram_matrix = jnp.einsum("nfkp,nfjp->nkj", morph, morph, preferred_element_type=jnp.float32)
        lip_sed = jnp.sqrt(jnp.sum(gram_matrix * gram_matrix, axis=(1, 2))) + 1.0
        gradient = jnp.einsum("nfkp,nfbp->nkb", morph, misfit, preferred_element_type=jnp.float32)
        sed = (
            jnp.maximum(sed.astype(jnp.float32) - gradient / lip_sed[:, None, None], 0.0)
            * active[:, :, None]
        ).astype(jnp.bfloat16)
        model = jnp.einsum("nkb,nfkp->nfbp", sed, morph, preferred_element_type=jnp.float32)
        misfit = (model - target).astype(jnp.bfloat16)
        sed_gram = jnp.einsum("nkb,nkc->nbc", sed, sed, preferred_element_type=jnp.float32)
        lip_morph = jnp.sqrt(jnp.sum(sed_gram * sed_gram, axis=(1, 2))) + 1.0
        grad_morph = jnp.einsum("nkb,nfbp->nfkp", sed, misfit, preferred_element_type=jnp.float32)
        morph = (
            jnp.maximum(morph - (grad_morph + 0.1) / lip_morph[:, None, None, None], 0.0)
            * active[:, None, :, None]
        ).astype(jnp.bfloat16)
    model_out = jnp.einsum("nkb,nfkp->nfbp", sed, morph, preferred_element_type=jnp.float32).astype(
        jnp.bfloat16
    )
    return (sed, morph, model_out)


def on_device(pixel_tiles, blend_source, blend_slot, component_count, sed_start, morph_start):
    peer_count = lax.axis_size("dev")
    blend_rows, footprint = blend_source.shape
    entries = blend_rows * footprint
    capacity = max(2, (entries + peer_count - 1) // peer_count)
    tile_rows, bands, pixels = pixel_tiles.shape
    sources = blend_source.reshape(entries)
    one_hot = (sources[:, None] == jnp.arange(peer_count, dtype=jnp.int32)[None, :]).astype(
        jnp.int32
    )
    ranking = jnp.sum((jnp.cumsum(one_hot, axis=0) - 1) * one_hot, axis=1)
    placing = sources * capacity + ranking
    asking = (
        jnp.zeros((peer_count * capacity,), jnp.int32)
        .at[placing]
        .set(blend_slot.reshape(entries) + 1)
    )
    wanted = lax.all_to_all(
        asking.reshape(peer_count, capacity), "dev", split_axis=0, concat_axis=0, tiled=True
    )
    source_rows = jnp.maximum(wanted - 1, 0).reshape(-1)
    filled = (wanted > 0).reshape(-1)
    outgoing = jnp.where(filled[:, None, None], pixel_tiles[source_rows], 0.0).astype(jnp.bfloat16)
    arrived = lax.all_to_all(
        outgoing.reshape(peer_count, capacity, bands, pixels),
        "dev",
        split_axis=0,
        concat_axis=0,
        tiled=True,
    )
    blend_data = arrived.reshape(peer_count * capacity, bands, pixels)[placing].reshape(
        blend_rows, footprint, bands, pixels
    )
    block_size = math.gcd(blend_rows, 8)
    groups = blend_rows // block_size

    def in_blocks(array):
        return array.reshape((groups, block_size) + array.shape[1:])

    sed_blocks, morph_blocks, model_blocks = lax.map(
        lambda inputs: fit_block(*inputs),
        (
            in_blocks(blend_data),
            in_blocks(sed_start),
            in_blocks(morph_start),
            in_blocks(component_count),
        ),
    )
    sed_final = sed_blocks.reshape(sed_start.shape)
    models = model_blocks.reshape(entries, bands, pixels)
    outbound = (
        jnp.zeros((peer_count * capacity, bands, pixels), jnp.bfloat16).at[placing].set(models)
    )
    returned = lax.all_to_all(
        outbound.reshape(peer_count, capacity, bands, pixels),
        "dev",
        split_axis=0,
        concat_axis=0,
        tiled=True,
    )
    returned = returned.reshape(peer_count * capacity, bands * pixels)
    selector = (
        (source_rows[None, :] == jnp.arange(tile_rows, dtype=jnp.int32)[:, None]) & filled[None, :]
    ).astype(jnp.bfloat16)
    summed = jnp.dot(selector, returned, preferred_element_type=jnp.float32).reshape(
        tile_rows, bands, pixels
    )
    residual = pixel_tiles - summed
    total_sq = lax.psum(jnp.sum(residual * residual), ("grp", "dev"))
    pixel_count = float(residual.size * lax.axis_size("grp") * peer_count)
    whitened = residual / jnp.sqrt(total_sq / pixel_count + 1e-06)
    return (whitened, sed_final)


def solution(mesh):
    placed = (
        P(("grp", "dev"), None, None),
        P(("grp", "dev"), None),
        P(("grp", "dev"), None),
        P(("grp", "dev")),
        P(("grp", "dev"), None, None),
        P(("grp", "dev"), None, None, None),
    )
    return jax.shard_map(
        on_device,
        mesh=mesh,
        in_specs=placed,
        out_specs=(P(("grp", "dev"), None, None), P(("grp", "dev"), None, None)),
        check_vma=False,
    )
```

profile of v0, /device:TPU:0, one launch (start us, length us, event | category | flops | bytes accessed | tf_op | source)
XLA Modules:
  0.0 175.2 jit_solution(13595546638823699439)
XLA Ops:
  4.9 15.4 %all_to_all.19 = s32[16,1,8]{2,1,0:T(1,128)S(1)} all-to-all(s32[16,1,8]{2,1,0:T(1,128)S(1)} %bitcast.322), channel_id=1, replica_groups=mesh['grp'=2,'dev'=16] {'dev'}, dimensions={0} | all-to-all | bytes 1024 | tf_op jit(solution)/shard_map/all_to_all | solution.py:59
  20.7 3.4 %gather_fusion = bf16[128,6,512]{2,0,1:T(8,128)(2,1)S(1)} fusion(f32[64,6,512]{2,0,1:T(8,128)} %param.8, s32[1024]{0:T(1024)S(1)} %pad_clamp_fusion.1), kind=kCustom, calls=%fused_computation | custom fusion | bytes 1573376 | tf_op jit(solution)/shard_map/gather | solution.py:64
  25.3 3.6 %all-to-all-start.1 = ((bf16[16,8,6,512]{3,1,2,0:T(8,128)(2,1)}), bf16[16,8,6,512]{3,1,2,0:T(8,128)(2,1)S(1)}, u32[]{:S(2)}, u32[]{:S(2)}) async-start(bf16[16,8,6,512]{3,1,2,0:T(8,128)(2,1)} %fusion.92), calls=%async_computation.1 | async-start | bytes 1572864 | tf_op jit(solution)/shard_map/all_to_all | solution.py:65
  29.2 18.2 %all-to-all-done.1 = bf16[16,8,6,512]{3,1,2,0:T(8,128)(2,1)S(1)} async-done(((bf16[16,8,6,512]{3,1,2,0:T(8,128)(2,1)}), bf16[16,8,6,512]{3,1,2,0:T(8,128)(2,1)S(1)}, u32[]{:S(2)}, u32[]{:S(2)}) %all-to-all-start.1) | async-done | bytes 786464 | tf_op jit(solution)/shard_map/all_to_all | solution.py:65
  48.4 54.7 %while.12 = (s32[]{:T(128)}, bf16[8,8,24,6]{2,3,1,0:T(8,128)(2,1)S(1)}, bf16[8,8,2,6,512]{4,3,2,1,0:T(8,128)(2,1)S(1)}, bf16[8,8,24,6]{2,3,1,0:T(8,128)(2,1)S(1)...) while((s32[]{:T(128)}, ...), condition=%wide.region_8.9_spmd, body=%wide.region_3.8_spmd.sunk | while | flops 44944320 | bytes 5388865 | solution.py:81
  48.5 1.6 fusion.163
  50.0 1.6 fusion.164
  51.9 1.7 fusion.166
  55.3 1.6 fusion.163
  56.9 1.6 fusion.164
  58.8 1.7 fusion.166
  65.6 1.6 fusion.166
  72.4 1.6 fusion.166
  79.2 1.6 fusion.166
  86.0 1.6 fusion.166
  89.4 1.6 fusion.163
  91.0 1.6 fusion.164
  92.8 1.7 fusion.166
  97.9 1.6 fusion.164
  99.7 1.6 fusion.166
  103.1 4.3 %scatter_fusion = bf16[128,6,512]{2,1,0:T(8,128)(2,1)S(1)} fusion(bf16[128,6,512]{2,1,0:T(8,128)(2,1)S(1)} %broadcast_in_dim.24, s32[128]{0:T(128)S(1)} %fusion.99, bf16[128,6,512]{2,1,0:T(8,128)(2,1)S(1)} %bitcast.319), kind=kCustom, calls=%fused_computation.3 | custom fusion | bytes 2359808 | tf_op jit(solution)/shard_map/scatter | solution.py:93
  108.6 4.9 %all-to-all-start.2 = ((bf16[16,8,6,512]{3,1,2,0:T(8,128)(2,1)}), bf16[16,8,6,512]{3,1,2,0:T(8,128)(2,1)S(1)}, u32[]{:S(2)}, u32[]{:S(2)}) async-start(bf16[16,8,6,512]{3,1,2,0:T(8,128)(2,1)} %copy.40), calls=%async_computation.2 | async-start | bytes 1572864 | tf_op jit(solution)/shard_map/all_to_all | solution.py:95
  114.5 17.6 %all-to-all-done.2 = bf16[16,8,6,512]{3,1,2,0:T(8,128)(2,1)S(1)} async-done(((bf16[16,8,6,512]{3,1,2,0:T(8,128)(2,1)}), bf16[16,8,6,512]{3,1,2,0:T(8,128)(2,1)S(1)}, u32[]{:S(2)}, u32[]{:S(2)}) %all-to-all-start.2) | async-done | bytes 786464 | tf_op jit(solution)/shard_map/all_to_all | solution.py:95
  133.5 40.0 %psum.7 = f32[]{:T(128)} all-reduce(f32[]{:T(128)} %get-tuple-element.64), channel_id=1, replica_groups=mesh['grp'=2,'dev'=16] {'grp','dev'}, use_global_device_ids=true, to_apply=%region_11.12 | all-reduce | flops 1 | bytes 8 | tf_op jit(solution)/shard_map/psum | solution.py:110
  (149 shorter events, 41.5 us)
Async XLA Ops:
  24.1 4.8 %copy-start.1 = (bf16[64,24,6]{0,1,2:T(8,128)(2,1)S(1)}, bf16[64,24,6]{0,1,2:T(8,128)(2,1)}, u32[]{:S(2)}) copy-start(bf16[64,24,6]{0,1,2:T(8,128)(2,1)} %param.12) | copy-start | bytes 55300
  24.1 5.0 %copy-start.2 = (s32[64]{0:T(128)S(1)}, s32[64]{0:T(128)}, u32[]{:S(2)}) copy-start(s32[64]{0:T(128)} %param.11) | copy-start | bytes 772
  25.3 22.1 %all-to-all-start.1 = ((bf16[16,8,6,512]{3,1,2,0:T(8,128)(2,1)}), bf16[16,8,6,512]{3,1,2,0:T(8,128)(2,1)S(1)}, u32[]{:S(2)}, u32[]{:S(2)}) async-start(bf16[16,8,6,512]{3,1,2,0:T(8,128)(2,1)} %fusion.92), calls=%async_computation.1 | async-start | bytes 1572864 | tf_op jit(solution)/shard_map/all_to_all | solution.py:65
  107.5 25.0 %copy-start = (f32[64,6,512]{2,0,1:T(8,128)S(1)}, f32[64,6,512]{2,0,1:T(8,128)}, u32[]{:S(2)}) copy-start(f32[64,6,512]{2,0,1:T(8,128)} %param.8) | copy-start | bytes 2359300
  108.6 23.5 %all-to-all-start.2 = ((bf16[16,8,6,512]{3,1,2,0:T(8,128)(2,1)}), bf16[16,8,6,512]{3,1,2,0:T(8,128)(2,1)S(1)}, u32[]{:S(2)}, u32[]{:S(2)}) async-start(bf16[16,8,6,512]{3,1,2,0:T(8,128)(2,1)} %copy.40), calls=%async_computation.2 | async-start | bytes 1572864 | tf_op jit(solution)/shard_map/all_to_all | solution.py:95
where the time goes:
time: 176 us; the launch traced here: 175 us
  blocking collectives  55.5 us (32%)
  matrix products  54.3 us (31%)
  waiting for transfers between devices  35.8 us (20%)
  local copies, waits for them, and re-layouts  14.3 us (8%)
  starting transfers between devices  8.54 us (5%)
  other arithmetic  4.83 us (3%)
    psum x1, blocking collectives, on_device(): total_sq = lax.psum(jnp.sum(residual * residual), ('grp', 'dev'))  40 us
    all_to_all x1, waiting for transfers between devices, on_device(): lax.all_to_all(outgoing.reshape(peer_count, capacity, bands, pixels), 'de...  18.2 us
    all_to_all x1, waiting for transfers between devices, on_device(): lax.all_to_all(outbound.reshape(peer_count, capacity, bands, pixels), 'de...  17.6 us
    all_to_all x1, blocking collectives, on_device(): lax.all_to_all(asking.reshape(peer_count, capacity), 'dev', split_axis=0,...  15.4 us
    dot_general x16, matrix products, fit_block(): jnp.einsum('nfkp,nfbp->nkb', morph, misfit, preferred_element_type=jnp.fl...  15.4 us
    dot_general x16, matrix products, fit_block(): jnp.einsum('nfkp,nfjp->nkj', morph, morph, preferred_element_type=jnp.flo...  15.2 us
    dot_general x8, matrix products, fit_block(): jnp.einsum('nkb,nfbp->nfkp', sed, misfit, preferred_element_type=jnp.floa...  13.2 us
    dot_general x16, matrix products, fit_block(): jnp.einsum('nkb,nfkp->nfbp', sed, morph, preferred_element_type=jnp.float32)  5.36 us
  transfers between devices with their start and end apart: 2, of which 2 were waited for; matrix products, arithmetic and copies ran while one was open for 1% of the time, Pallas kernels for 0%

commit v1 on v0

--- a/solution.py
+++ b/solution.py
@@ -107,7 +107,10 @@
         tile_rows, bands, pixels
     )
     residual = pixel_tiles - summed
-    total_sq = lax.psum(jnp.sum(residual * residual), ("grp", "dev"))
+    everyone = lax.axis_size("grp") * peer_count
+    partial = jnp.broadcast_to(jnp.sum(residual * residual), (everyone, 1, 128))
+    partials = lax.all_to_all(partial, ("grp", "dev"), split_axis=0, concat_axis=0, tiled=True)
+    total_sq = jnp.sum(partials[:, 0, 0])
     pixel_count = float(residual.size * lax.axis_size("grp") * peer_count)
     whitened = residual / jnp.sqrt(total_sq / pixel_count + 1e-06)
     return (whitened, sed_final)

time: 176 us -> 149 us (0.85)
  blocking collectives: 55.5 us -> 15.4 us
  waiting for transfers between devices: 35.8 us -> 42.9 us
  starting transfers between devices: 8.54 us -> 12.5 us
    psum x1 -> x0, blocking collectives: 40 us -> none  [on_device(): total_sq = lax.psum(jnp.sum(residual * residual), ('grp', 'dev'))]
    all_to_all x0 -> x1, waiting for transfers between devices: none -> 6.34 us  [on_device(): lax.all_to_all(partial, ('grp', 'dev'), split_axis=0, concat_axis=0, tile...]
    all_to_all x0 -> x1, starting transfers between devices: none -> 3.94 us  [on_device(): lax.all_to_all(partial, ('grp', 'dev'), split_axis=0, concat_axis=0, tile...]
  transfers between devices with their start and end apart: 2 -> 3, of which waited for: 2 -> 3; matrix products, arithmetic and copies ran while one was open for 1% -> 1% of each run, Pallas kernels for 0% -> 0%
where the time goes in v1:
time: 149 us; the launch traced here: 148 us
  matrix products  54.3 us (36%)
  waiting for transfers between devices  42.9 us (29%)
  local copies, waits for them, and re-layouts  15.5 us (10%)
  blocking collectives  15.4 us (10%)
  starting transfers between devices  12.5 us (8%)
  other arithmetic  5.47 us (4%)
  between operations  1.53 us (1%)
    all_to_all x1, waiting for transfers between devices, on_device(): lax.all_to_all(outbound.reshape(peer_count, capacity, bands, pixels), 'de...  18.3 us
    all_to_all x1, waiting for transfers between devices, on_device(): lax.all_to_all(outgoing.reshape(peer_count, capacity, bands, pixels), 'de...  18.2 us
    all_to_all x1, blocking collectives, on_device(): lax.all_to_all(asking.reshape(peer_count, capacity), 'dev', split_axis=0,...  15.4 us
    dot_general x16, matrix products, fit_block(): jnp.einsum('nfkp,nfbp->nkb', morph, misfit, preferred_element_type=jnp.fl...  15.4 us
    dot_general x16, matrix products, fit_block(): jnp.einsum('nfkp,nfjp->nkj', morph, morph, preferred_element_type=jnp.flo...  15.2 us
    dot_general x8, matrix products, fit_block(): jnp.einsum('nkb,nfbp->nfkp', sed, misfit, preferred_element_type=jnp.floa...  13.2 us
    all_to_all x1, waiting for transfers between devices, on_device(): lax.all_to_all(partial, ('grp', 'dev'), split_axis=0, concat_axis=0, tile...  6.34 us
    dot_general x16, matrix products, fit_block(): jnp.einsum('nkb,nfkp->nfbp', sed, morph, preferred_element_type=jnp.float32)  5.34 us
  transfers between devices with their start and end apart: 3, of which 3 were waited for; matrix products, arithmetic and copies ran while one was open for 1% of the time, Pallas kernels for 0%

profile of v1, /device:TPU:0, one launch (start us, length us, event | category | flops | bytes accessed | tf_op | source)
XLA Modules:
  0.0 148.1 jit_solution(11817741575304413354)
XLA Ops:
  4.9 15.4 %all_to_all.24 = s32[16,1,8]{2,1,0:T(1,128)S(1)} all-to-all(s32[16,1,8]{2,1,0:T(1,128)S(1)} %bitcast.322), channel_id=1, replica_groups=mesh['grp'=2,'dev'=16] {'dev'}, dimensions={0} | all-to-all | bytes 1024 | tf_op jit(solution)/shard_map/all_to_all | solution.py:59
  20.7 3.4 %gather_fusion = bf16[128,6,512]{2,0,1:T(8,128)(2,1)S(1)} fusion(f32[64,6,512]{2,0,1:T(8,128)} %param.8, s32[1024]{0:T(1024)S(1)} %pad_clamp_fusion.1), kind=kCustom, calls=%fused_computation | custom fusion | bytes 1573376 | tf_op jit(solution)/shard_map/gather | solution.py:64
  25.3 3.6 %all-to-all-start.1 = ((bf16[16,8,6,512]{3,1,2,0:T(8,128)(2,1)}), bf16[16,8,6,512]{3,1,2,0:T(8,128)(2,1)S(1)}, u32[]{:S(2)}, u32[]{:S(2)}) async-start(bf16[16,8,6,512]{3,1,2,0:T(8,128)(2,1)} %fusion.92), calls=%async_computation.1 | async-start | bytes 1572864 | tf_op jit(solution)/shard_map/all_to_all | solution.py:65
  29.2 18.2 %all-to-all-done.1 = bf16[16,8,6,512]{3,1,2,0:T(8,128)(2,1)S(1)} async-done(((bf16[16,8,6,512]{3,1,2,0:T(8,128)(2,1)}), bf16[16,8,6,512]{3,1,2,0:T(8,128)(2,1)S(1)}, u32[]{:S(2)}, u32[]{:S(2)}) %all-to-all-start.1) | async-done | bytes 786464 | tf_op jit(solution)/shard_map/all_to_all | solution.py:65
  48.4 54.7 %while.12 = (s32[]{:T(128)}, bf16[8,8,24,6]{2,3,1,0:T(8,128)(2,1)S(1)}, bf16[8,8,2,6,512]{4,3,2,1,0:T(8,128)(2,1)S(1)}, bf16[8,8,24,6]{2,3,1,0:T(8,128)(2,1)S(1)...) while((s32[]{:T(128)}, ...), condition=%wide.region_8.9_spmd, body=%wide.region_3.8_spmd.sunk | while | flops 44944320 | bytes 5388865 | solution.py:81
  50.1 1.6 %fusion.164 = bf16[8,24,6]{1,2,0:T(8,128)(2,1)S(1)} fusion(bf16[8,8,2,24,512]{4,3,2,1,0:T(8,128)(2,1)} %get-tuple-element.142, s32[]{:T(128)} %get-tuple-element.129, bf16[8,24]{1,0:T(8,128)(2,1)S(1)} %get-tuple-element.118, bf16[8,8,2,6,512]{4,3,2,1,0:T(8,128)(2,1)S(1)} %get-tuple-element.143, f32[8]{0:T(128)S(1)} %sqrt_add_fusion.8, ...), kind=kOutput, calls=%fused_computation.57.clone.1 | convolution fusion | flops 5273088 | bytes 967936 | tf_op jit(solution)/shard_map/while/body/eval_jaxpr/nfkp,nfbp->nkb/dot_general | solution.py:22
  51.9 1.7 %fusion.166 = bf16[8,2,24,512]{3,2,1,0:T(8,128)(2,1)S(1)} fusion(f32[8,24]{1,0:T(8,128)S(1)} %get-tuple-element.117, f32[8]{0:T(128)S(1)} %sqrt_add_fusion.9, bf16[8,8,2,24,512]{4,3,2,1,0:T(8,128)(2,1)} %get-tuple-element.142, s32[]{:T(128)} %get-tuple-element.129, bf16[8,24]{1,0:T(8,128)(2,1)S(1)} %get-tuple-element.118, ...), kind=kOutput, calls=%fused_computation.16.clone.1 | convolution fusion | flops 7028736 | bytes 1353728 | tf_op jit(solution)/shard_map/while/body/eval_jaxpr/nkb,nfbp->nfkp/dot_general | solution.py:31
  55.3 1.6 %fusion.163 = f32[8]{0:T(128)S(1)} fusion(bf16[8,8,2,24,512]{4,3,2,1,0:T(8,128)(2,1)} %get-tuple-element.142, s32[]{:T(128)} %get-tuple-element.129, bf16[8,24]{1,0:T(8,128)(2,1)S(1)} %get-tuple-element.118), kind=kOutput, calls=%fused_computation.40.clone.1 | convolution fusion | flops 9643000 | bytes 394144 | tf_op jit(solution)/shard_map/while/body/eval_jaxpr/nfkp,nfjp->nkj/dot_general | solution.py:20
  56.9 1.6 %fusion.164 = bf16[8,24,6]{1,2,0:T(8,128)(2,1)S(1)} fusion(bf16[8,8,2,24,512]{4,3,2,1,0:T(8,128)(2,1)} %get-tuple-element.142, s32[]{:T(128)} %get-tuple-element.129, bf16[8,24]{1,0:T(8,128)(2,1)S(1)} %get-tuple-element.118, bf16[8,8,2,6,512]{4,3,2,1,0:T(8,128)(2,1)S(1)} %get-tuple-element.143, f32[8]{0:T(128)S(1)} %sqrt_add_fusion.8, ...), kind=kOutput, calls=%fused_computation.57.clone.1 | convolution fusion | flops 5273088 | bytes 967936 | tf_op jit(solution)/shard_map/while/body/eval_jaxpr/nfkp,nfbp->nkb/dot_general | solution.py:22
  58.8 1.7 %fusion.166 = bf16[8,2,24,512]{3,2,1,0:T(8,128)(2,1)S(1)} fusion(f32[8,24]{1,0:T(8,128)S(1)} %get-tuple-element.117, f32[8]{0:T(128)S(1)} %sqrt_add_fusion.9, bf16[8,8,2,24,512]{4,3,2,1,0:T(8,128)(2,1)} %get-tuple-element.142, s32[]{:T(128)} %get-tuple-element.129, bf16[8,24]{1,0:T(8,128)(2,1)S(1)} %get-tuple-element.118, ...), kind=kOutput, calls=%fused_computation.16.clone.1 | convolution fusion | flops 7028736 | bytes 1353728 | tf_op jit(solution)/shard_map/while/body/eval_jaxpr/nkb,nfbp->nfkp/dot_general | solution.py:31
  65.6 1.6 %fusion.166 = bf16[8,2,24,512]{3,2,1,0:T(8,128)(2,1)S(1)} fusion(f32[8,24]{1,0:T(8,128)S(1)} %get-tuple-element.117, f32[8]{0:T(128)S(1)} %sqrt_add_fusion.9, bf16[8,8,2,24,512]{4,3,2,1,0:T(8,128)(2,1)} %get-tuple-element.142, s32[]{:T(128)} %get-tuple-element.129, bf16[8,24]{1,0:T(8,128)(2,1)S(1)} %get-tuple-element.118, ...), kind=kOutput, calls=%fused_computation.16.clone.1 | convolution fusion | flops 7028736 | bytes 1353728 | tf_op jit(solution)/shard_map/while/body/eval_jaxpr/nkb,nfbp->nfkp/dot_general | solution.py:31
  72.4 1.6 %fusion.166 = bf16[8,2,24,512]{3,2,1,0:T(8,128)(2,1)S(1)} fusion(f32[8,24]{1,0:T(8,128)S(1)} %get-tuple-element.117, f32[8]{0:T(128)S(1)} %sqrt_add_fusion.9, bf16[8,8,2,24,512]{4,3,2,1,0:T(8,128)(2,1)} %get-tuple-element.142, s32[]{:T(128)} %get-tuple-element.129, bf16[8,24]{1,0:T(8,128)(2,1)S(1)} %get-tuple-element.118, ...), kind=kOutput, calls=%fused_computation.16.clone.1 | convolution fusion | flops 7028736 | bytes 1353728 | tf_op jit(solution)/shard_map/while/body/eval_jaxpr/nkb,nfbp->nfkp/dot_general | solution.py:31
  79.2 1.6 %fusion.166 = bf16[8,2,24,512]{3,2,1,0:T(8,128)(2,1)S(1)} fusion(f32[8,24]{1,0:T(8,128)S(1)} %get-tuple-element.117, f32[8]{0:T(128)S(1)} %sqrt_add_fusion.9, bf16[8,8,2,24,512]{4,3,2,1,0:T(8,128)(2,1)} %get-tuple-element.142, s32[]{:T(128)} %get-tuple-element.129, bf16[8,24]{1,0:T(8,128)(2,1)S(1)} %get-tuple-element.118, ...), kind=kOutput, calls=%fused_computation.16.clone.1 | convolution fusion | flops 7028736 | bytes 1353728 | tf_op jit(solution)/shard_map/while/body/eval_jaxpr/nkb,nfbp->nfkp/dot_general | solution.py:31
  86.0 1.6 %fusion.166 = bf16[8,2,24,512]{3,2,1,0:T(8,128)(2,1)S(1)} fusion(f32[8,24]{1,0:T(8,128)S(1)} %get-tuple-element.117, f32[8]{0:T(128)S(1)} %sqrt_add_fusion.9, bf16[8,8,2,24,512]{4,3,2,1,0:T(8,128)(2,1)} %get-tuple-element.142, s32[]{:T(128)} %get-tuple-element.129, bf16[8,24]{1,0:T(8,128)(2,1)S(1)} %get-tuple-element.118, ...), kind=kOutput, calls=%fused_computation.16.clone.1 | convolution fusion | flops 7028736 | bytes 1353728 | tf_op jit(solution)/shard_map/while/body/eval_jaxpr/nkb,nfbp->nfkp/dot_general | solution.py:31
  89.4 1.6 %fusion.163 = f32[8]{0:T(128)S(1)} fusion(bf16[8,8,2,24,512]{4,3,2,1,0:T(8,128)(2,1)} %get-tuple-element.142, s32[]{:T(128)} %get-tuple-element.129, bf16[8,24]{1,0:T(8,128)(2,1)S(1)} %get-tuple-element.118), kind=kOutput, calls=%fused_computation.40.clone.1 | convolution fusion | flops 9643000 | bytes 394144 | tf_op jit(solution)/shard_map/while/body/eval_jaxpr/nfkp,nfjp->nkj/dot_general | solution.py:20
  91.0 1.6 %fusion.164 = bf16[8,24,6]{1,2,0:T(8,128)(2,1)S(1)} fusion(bf16[8,8,2,24,512]{4,3,2,1,0:T(8,128)(2,1)} %get-tuple-element.142, s32[]{:T(128)} %get-tuple-element.129, bf16[8,24]{1,0:T(8,128)(2,1)S(1)} %get-tuple-element.118, bf16[8,8,2,6,512]{4,3,2,1,0:T(8,128)(2,1)S(1)} %get-tuple-element.143, f32[8]{0:T(128)S(1)} %sqrt_add_fusion.8, ...), kind=kOutput, calls=%fused_computation.57.clone.1 | convolution fusion | flops 5273088 | bytes 967936 | tf_op jit(solution)/shard_map/while/body/eval_jaxpr/nfkp,nfbp->nkb/dot_general | solution.py:22
  92.8 1.7 %fusion.166 = bf16[8,2,24,512]{3,2,1,0:T(8,128)(2,1)S(1)} fusion(f32[8,24]{1,0:T(8,128)S(1)} %get-tuple-element.117, f32[8]{0:T(128)S(1)} %sqrt_add_fusion.9, bf16[8,8,2,24,512]{4,3,2,1,0:T(8,128)(2,1)} %get-tuple-element.142, s32[]{:T(128)} %get-tuple-element.129, bf16[8,24]{1,0:T(8,128)(2,1)S(1)} %get-tuple-element.118, ...), kind=kOutput, calls=%fused_computation.16.clone.1 | convolution fusion | flops 7028736 | bytes 1353728 | tf_op jit(solution)/shard_map/while/body/eval_jaxpr/nkb,nfbp->nfkp/dot_general | solution.py:31
  97.9 1.6 %fusion.164 = bf16[8,24,6]{1,2,0:T(8,128)(2,1)S(1)} fusion(bf16[8,8,2,24,512]{4,3,2,1,0:T(8,128)(2,1)} %get-tuple-element.142, s32[]{:T(128)} %get-tuple-element.129, bf16[8,24]{1,0:T(8,128)(2,1)S(1)} %get-tuple-element.118, bf16[8,8,2,6,512]{4,3,2,1,0:T(8,128)(2,1)S(1)} %get-tuple-element.143, f32[8]{0:T(128)S(1)} %sqrt_add_fusion.8, ...), kind=kOutput, calls=%fused_computation.57.clone.1 | convolution fusion | flops 5273088 | bytes 967936 | tf_op jit(solution)/shard_map/while/body/eval_jaxpr/nfkp,nfbp->nkb/dot_general | solution.py:22
  99.7 1.6 %fusion.166 = bf16[8,2,24,512]{3,2,1,0:T(8,128)(2,1)S(1)} fusion(f32[8,24]{1,0:T(8,128)S(1)} %get-tuple-element.117, f32[8]{0:T(128)S(1)} %sqrt_add_fusion.9, bf16[8,8,2,24,512]{4,3,2,1,0:T(8,128)(2,1)} %get-tuple-element.142, s32[]{:T(128)} %get-tuple-element.129, bf16[8,24]{1,0:T(8,128)(2,1)S(1)} %get-tuple-element.118, ...), kind=kOutput, calls=%fused_computation.16.clone.1 | convolution fusion | flops 7028736 | bytes 1353728 | tf_op jit(solution)/shard_map/while/body/eval_jaxpr/nkb,nfbp->nfkp/dot_general | solution.py:31
  103.1 4.3 %scatter_fusion = bf16[128,6,512]{2,1,0:T(8,128)(2,1)S(1)} fusion(bf16[128,6,512]{2,1,0:T(8,128)(2,1)S(1)} %broadcast_in_dim.26, s32[128]{0:T(128)S(1)} %fusion.99, bf16[128,6,512]{2,1,0:T(8,128)(2,1)S(1)} %bitcast.319), kind=kCustom, calls=%fused_computation.3 | custom fusion | bytes 2359808 | tf_op jit(solution)/shard_map/scatter | solution.py:93
  108.7 4.9 %all-to-all-start.2 = ((bf16[16,8,6,512]{3,1,2,0:T(8,128)(2,1)}), bf16[16,8,6,512]{3,1,2,0:T(8,128)(2,1)S(1)}, u32[]{:S(2)}, u32[]{:S(2)}) async-start(bf16[16,8,6,512]{3,1,2,0:T(8,128)(2,1)} %copy.74), calls=%async_computation.2 | async-start | bytes 1572864 | tf_op jit(solution)/shard_map/all_to_all | solution.py:95
  113.8 18.3 %all-to-all-done.2 = bf16[16,8,6,512]{3,1,2,0:T(8,128)(2,1)S(1)} async-done(((bf16[16,8,6,512]{3,1,2,0:T(8,128)(2,1)}), bf16[16,8,6,512]{3,1,2,0:T(8,128)(2,1)S(1)}, u32[]{:S(2)}, u32[]{:S(2)}) %all-to-all-start.2) | async-done | bytes 786464 | tf_op jit(solution)/shard_map/all_to_all | solution.py:95
  134.8 3.9 %all-to-all-start.3 = ((f32[32,1,128]{2,1,0:T(1,128)}), f32[32,1,128]{2,1,0:T(1,128)S(1)}, u32[]{:S(2)}, u32[]{:S(2)}) async-start(f32[32,1,128]{2,1,0:T(1,128)} %broadcast_in_dim.45), calls=%async_computation.3 | async-start | bytes 32768 | tf_op jit(solution)/shard_map/all_to_all | solution.py:112
  139.5 6.3 %all-to-all-done.3 = f32[32,1,128]{2,1,0:T(1,128)S(1)} async-done(((f32[32,1,128]{2,1,0:T(1,128)}), f32[32,1,128]{2,1,0:T(1,128)S(1)}, u32[]{:S(2)}, u32[]{:S(2)}) %all-to-all-start.3) | async-done | bytes 16416 | tf_op jit(solution)/shard_map/all_to_all | solution.py:112
  (152 shorter events, 45.0 us)
Async XLA Ops:
  24.1 4.8 %copy-start.1 = (bf16[64,24,6]{0,1,2:T(8,128)(2,1)S(1)}, bf16[64,24,6]{0,1,2:T(8,128)(2,1)}, u32[]{:S(2)}) copy-start(bf16[64,24,6]{0,1,2:T(8,128)(2,1)} %param.12) | copy-start | bytes 55300
  24.1 5.0 %copy-start.2 = (s32[64]{0:T(128)S(1)}, s32[64]{0:T(128)}, u32[]{:S(2)}) copy-start(s32[64]{0:T(128)} %param.11) | copy-start | bytes 772
  25.3 22.1 %all-to-all-start.1 = ((bf16[16,8,6,512]{3,1,2,0:T(8,128)(2,1)}), bf16[16,8,6,512]{3,1,2,0:T(8,128)(2,1)S(1)}, u32[]{:S(2)}, u32[]{:S(2)}) async-start(bf16[16,8,6,512]{3,1,2,0:T(8,128)(2,1)} %fusion.92), calls=%async_computation.1 | async-start | bytes 1572864 | tf_op jit(solution)/shard_map/all_to_all | solution.py:65
  107.5 25.0 %copy-start = (f32[64,6,512]{2,0,1:T(8,128)S(1)}, f32[64,6,512]{2,0,1:T(8,128)}, u32[]{:S(2)}) copy-start(f32[64,6,512]{2,0,1:T(8,128)} %param.8) | copy-start | bytes 2359300
  108.7 23.4 %all-to-all-start.2 = ((bf16[16,8,6,512]{3,1,2,0:T(8,128)(2,1)}), bf16[16,8,6,512]{3,1,2,0:T(8,128)(2,1)S(1)}, u32[]{:S(2)}, u32[]{:S(2)}) async-start(bf16[16,8,6,512]{3,1,2,0:T(8,128)(2,1)} %copy.74), calls=%async_computation.2 | async-start | bytes 1572864 | tf_op jit(solution)/shard_map/all_to_all | solution.py:95
  134.8 11.0 %all-to-all-start.3 = ((f32[32,1,128]{2,1,0:T(1,128)}), f32[32,1,128]{2,1,0:T(1,128)S(1)}, u32[]{:S(2)}, u32[]{:S(2)}) async-start(f32[32,1,128]{2,1,0:T(1,128)} %broadcast_in_dim.45), calls=%async_computation.3 | async-start | bytes 32768 | tf_op jit(solution)/shard_map/all_to_all | solution.py:112

commit v2 on v1

v2 whole, which is shorter than its diff:
```python
import functools
import math

import jax
import jax.numpy as jnp
from jax import lax
from jax.experimental import pallas as pl
from jax.experimental.pallas import tpu as pltpu
from jax.sharding import PartitionSpec as P

ITERS = 2
LANES = 8
F32 = jnp.float32
BF16 = jnp.bfloat16


def dot(left, right, left_dim, right_dim):
    return lax.dot_general(
        left, right, (((left_dim,), (right_dim,)), ((), ())), preferred_element_type=F32
    )


def inverse_lip(squares, components):
    rows, width = squares.shape
    total = jnp.sum(
        jnp.sum(squares.reshape(rows // components, components, width), axis=1),
        axis=1,
        keepdims=True,
    )
    inverse = 1.0 / (jnp.sqrt(total) + 1.0)
    return jnp.concatenate(
        [jnp.broadcast_to(inverse[n : n + 1], (components, 1)) for n in range(rows // components)],
        axis=0,
    )


def place_kernel(source_ref, slot_ref, asking_ref, placing_ref):
    peers, capacity = asking_ref.shape
    entries = source_ref.shape[1]
    peer = lax.broadcasted_iota(jnp.int32, (peers, entries), 0)
    named = peer == source_ref[...]
    before = lax.broadcasted_iota(jnp.int32, (entries, entries), 0)
    after = lax.broadcasted_iota(jnp.int32, (entries, entries), 1)
    upto = (before <= after).astype(F32).astype(BF16)
    rank = dot(named.astype(F32).astype(BF16), upto, 1, 0).astype(jnp.int32) - 1
    placing_ref[...] = jnp.sum(jnp.where(named, peer * capacity + rank, 0), axis=0, keepdims=True)
    value = jnp.broadcast_to(slot_ref[...] + 1, (peers, entries))
    for s in range(capacity):
        hit = jnp.where(named & (rank == s), value, 0)
        asking_ref[:, s : s + 1] = jnp.sum(hit, axis=1, keepdims=True)


def fit_kernel(
    count_ref, placing_ref, arrived_ref, sed_ref, morph_ref, sed_out_ref, out_ref,
    x_ref, mask_ref, data_ref, model_ref, *, units,
):
    step = pl.program_id(0)
    bands, slots, pixels = arrived_ref.shape
    entries = placing_ref.shape[1]
    footprint, components = morph_ref.shape[1:3]
    blends = entries // footprint
    rows = LANES * components
    cols = LANES * bands
    depth = x_ref.shape[1]

    def permutation():
        slot = lax.broadcasted_iota(jnp.int32, (slots, entries), 0)
        return (slot == placing_ref[...]).astype(F32).astype(BF16)

    @pl.when(step == 0)
    def _():
        chosen = permutation()
        for b in range(bands):
            data_ref[b] = dot(chosen, arrived_ref[b], 0, 0)
        lane = lax.broadcasted_iota(jnp.int32, (components, depth), 1)
        for n in range(LANES):
            own = (lane >= components * n) & (lane < components * (n + 1))
            side = (lane >= rows) & (lane < rows + cols) & (((lane - rows) & (LANES - 1)) == n)
            mask_ref[components * n : components * (n + 1), :] = (own | side).astype(F32)

    mask = mask_ref[...]
    in_gram = lax.broadcasted_iota(jnp.int32, (rows, depth), 1) < rows
    eye_row = lax.broadcasted_iota(jnp.int32, (depth - rows, cols), 0)
    eye_col = lax.broadcasted_iota(jnp.int32, (depth - rows, cols), 1)
    minus_eye = jnp.where(eye_row == eye_col, -1.0, 0.0)
    column = lax.broadcasted_iota(jnp.int32, (components, cols), 1)
    component = lax.broadcasted_iota(jnp.int32, (components, cols), 0)
    level = lax.broadcasted_iota(jnp.int32, (components, footprint * pixels), 0)
    seds = []
    for u in range(units):
        first = (step * units + u) * LANES
        counts = [count_ref[first + n] for n in range(LANES)]
        start = sed_ref[u].astype(F32)
        seds.append(
            jnp.concatenate(
                [
                    jnp.where(((column & (LANES - 1)) == n) & (component < counts[n]), start, 0.0)
                    for n in range(LANES)
                ],
                axis=0,
            )
        )
        morph = jnp.concatenate(
            [
                jnp.where(
                    level < counts[n],
                    jnp.concatenate(
                        [morph_ref[u * LANES + n, f].astype(F32) for f in range(footprint)], axis=1
                    ),
                    0.0,
                )
                for n in range(LANES)
            ],
            axis=0,
        )
        x_ref[u, 0:rows, :] = morph.astype(BF16)
        data = jnp.concatenate(
            [
                jnp.concatenate(
                    [
                        data_ref[b, pl.ds(pl.multiple_of(f * blends + first, LANES), LANES), :]
                        for f in range(footprint)
                    ],
                    axis=1,
                )
                for b in range(bands)
            ]
            + [jnp.zeros((depth - rows - cols, footprint * pixels), F32)],
            axis=0,
        )
        x_ref[u, rows:depth, :] = data.astype(BF16)
    for sweep in range(ITERS):
        grams = [dot(x_ref[u, 0:rows, :], x_ref[u], 1, 1) * mask for u in range(units)]
        for u in range(units):
            inverse = inverse_lip(jnp.where(in_gram, grams[u] * grams[u], 0.0), components)
            right = jnp.concatenate([seds[u], minus_eye], axis=0).astype(BF16)
            high = grams[u].astype(BF16)
            low = (grams[u] - high.astype(F32)).astype(BF16)
            gradient = dot(high, right, 1, 0) + dot(low, right, 1, 0)
            seds[u] = jnp.maximum(seds[u] - gradient * inverse, 0.0).astype(BF16).astype(F32)
        for u in range(units):
            right = jnp.concatenate([seds[u], minus_eye], axis=0).astype(BF16)
            left = dot(seds[u].astype(BF16), right, 1, 1)
            inverse = inverse_lip(jnp.where(in_gram, left * left, 0.0), components)
            gradient = dot(left.astype(BF16), x_ref[u], 1, 0)
            morph = x_ref[u, 0:rows, :].astype(F32)
            morph = jnp.maximum(morph - (gradient + 0.1) * inverse, 0.0)
            x_ref[u, 0:rows, :] = morph.astype(BF16)
    for u in range(units):
        first = (step * units + u) * LANES
        model = dot(seds[u].astype(BF16), x_ref[u, 0:rows, :], 0, 0)
        for b in range(bands):
            for f in range(footprint):
                model_ref[b, pl.ds(pl.multiple_of(f * blends + first, LANES), LANES), :] = model[
                    LANES * b : LANES * (b + 1), pixels * f : pixels * (f + 1)
                ]
        sed_out_ref[u] = jnp.sum(seds[u].reshape(LANES, components, cols), axis=0).astype(BF16)

    @pl.when(step == pl.num_programs(0) - 1)
    def _():
        chosen = permutation()
        for b in range(bands):
            out_ref[b] = dot(chosen, model_ref[b].astype(BF16), 1, 0).astype(BF16)


def on_device(pixel_tiles, blend_source, blend_slot, component_count, sed_start, morph_start):
    peer_count = lax.axis_size("dev")
    blend_rows, footprint = blend_source.shape
    components, bands = sed_start.shape[1:]
    entries = blend_rows * footprint
    capacity = max(2, (entries + peer_count - 1) // peer_count)
    slots = peer_count * capacity
    tile_rows, bands, pixels = pixel_tiles.shape
    asking, placing = pl.pallas_call(
        place_kernel,
        out_shape=(
            jax.ShapeDtypeStruct((peer_count, capacity), jnp.int32),
            jax.ShapeDtypeStruct((1, entries), jnp.int32),
        ),
        name="place",
    )(blend_source.T.reshape(1, entries), blend_slot.T.reshape(1, entries))
    wanted = lax.all_to_all(asking, "dev", split_axis=0, concat_axis=0, tiled=True).reshape(slots)
    selector = (
        wanted[None, :] == jnp.arange(1, tile_rows + 1, dtype=jnp.int32)[:, None]
    ).astype(BF16)
    outgoing = jnp.einsum(
        "ts,tbp->bsp", selector, pixel_tiles.astype(BF16), preferred_element_type=F32
    ).astype(BF16)

    def exchange(tiles):
        wire = tiles.reshape(bands, peer_count, capacity, pixels).transpose(1, 2, 0, 3)
        moved = lax.all_to_all(wire, "dev", split_axis=0, concat_axis=0, tiled=True)
        return moved.transpose(2, 0, 1, 3).reshape(bands, slots, pixels)

    arrived = exchange(outgoing)
    groups = blend_rows // LANES
    units = math.gcd(groups, 2)
    rows, cols = LANES * components, LANES * bands
    depth = -(-(rows + cols) // 128) * 128
    sed_in = (
        sed_start.reshape(groups, LANES, components, bands)
        .transpose(0, 2, 3, 1)
        .reshape(groups, components, cols)
    )
    sed_blocks, models = pl.pallas_call(
        functools.partial(fit_kernel, units=units),
        grid=(groups // units,),
        in_specs=[
            pl.BlockSpec(memory_space=pltpu.SMEM),
            pl.BlockSpec((1, entries), lambda i: (0, 0)),
            pl.BlockSpec((bands, slots, pixels), lambda i: (0, 0, 0)),
            pl.BlockSpec((units, components, cols), lambda i: (i, 0, 0)),
            pl.BlockSpec((units * LANES, footprint, components, pixels), lambda i: (i, 0, 0, 0)),
        ],
        out_specs=[
            pl.BlockSpec((units, components, cols), lambda i: (i, 0, 0)),
            pl.BlockSpec((bands, slots, pixels), lambda i: (0, 0, 0)),
        ],
        out_shape=(
            jax.ShapeDtypeStruct((groups, components, cols), BF16),
            jax.ShapeDtypeStruct((bands, slots, pixels), BF16),
        ),
        scratch_shapes=[
            pltpu.VMEM((units, depth, footprint * pixels), BF16),
            pltpu.VMEM((rows, depth), F32),
            pltpu.VMEM((bands, entries, pixels), F32),
            pltpu.VMEM((bands, entries, pixels), F32),
        ],
        compiler_params=pltpu.CompilerParams(dimension_semantics=("arbitrary",)),
        name="fit",
    )(component_count, placing, arrived, sed_in, morph_start)
    sed_final = (
        sed_blocks.reshape(groups, components, bands, LANES)
        .transpose(0, 3, 1, 2)
        .reshape(sed_start.shape)
    )
    returned = exchange(models)
    summed = jnp.einsum("ts,bsp->tbp", selector, returned, preferred_element_type=F32)
    residual = pixel_tiles - summed
    everyone = lax.axis_size("grp") * peer_count
    partial = jnp.broadcast_to(jnp.sum(residual * residual), (everyone, 1, 128))
    partials = lax.all_to_all(partial, ("grp", "dev"), split_axis=0, concat_axis=0, tiled=True)
    total_sq = jnp.sum(partials[:, 0, 0])
    pixel_count = float(residual.size * everyone)
    whitened = residual / jnp.sqrt(total_sq / pixel_count + 1e-06)
    return (whitened, sed_final)


def solution(mesh):
    placed = (
        P(("grp", "dev"), None, None),
        P(("grp", "dev"), None),
        P(("grp", "dev"), None),
        P(("grp", "dev")),
        P(("grp", "dev"), None, None),
        P(("grp", "dev"), None, None, None),
    )
    return jax.shard_map(
        on_device,
        mesh=mesh,
        in_specs=placed,
        out_specs=(P(("grp", "dev"), None, None), P(("grp", "dev"), None, None)),
        check_vma=False,
    )
```

time: 149 us -> 104 us (0.70)
  matrix products: 54.3 us -> 2.63 us
  Pallas kernels: 0 us -> 16.3 us
  blocking collectives: 15.4 us -> 0 us
  starting transfers between devices: 12.5 us -> 20.8 us
  waiting for transfers between devices: 42.9 us -> 49.6 us
  local copies, waits for them, and re-layouts: 15.5 us -> 10.1 us
  other arithmetic: 5.47 us -> 2.27 us
    dot_general x73 -> x2, matrix products: 54.3 us -> 2.63 us  [the longest x1 1.62 us: on_device(): jnp.einsum('ts,tbp->bsp', selector, pixel_tiles.astype(BF16), preferred_e...]
    pallas_call x0 -> x2, Pallas kernels: none -> 16.3 us  [the longest x1 14.8 us: on_device(): pl.pallas_call(functools.partial(fit_kernel, units=units), grid=(groups /...]
    all_to_all x1 -> x0, blocking collectives: 15.4 us -> none  [on_device(): lax.all_to_all(asking.reshape(peer_count, capacity), 'dev', split_axis=0,...]
    all_to_all x2 -> x3, starting transfers between devices: 8.52 us -> 16.9 us  [the longest x2 8.51 us: exchange(): moved = lax.all_to_all(wire, 'dev', split_axis=0, concat_axis=0, tiled=True)]
    all_to_all x2 -> x3, waiting for transfers between devices: 36.6 us -> 43.3 us  [the longest x2 36 us: exchange(): moved = lax.all_to_all(wire, 'dev', split_axis=0, concat_axis=0, tiled=True)]
    scatter x2 -> x0, local copies, waits for them, and re-layouts: 5.31 us -> none  [the longest x1 4.33 us: on_device(): jnp.zeros((peer_count * capacity, bands, pixels), jnp.bfloat16).at[placing]]
    gather x2 -> x0, local copies, waits for them, and re-layouts: 4.06 us -> none  [the longest x1 3.41 us: on_device(): pixel_tiles[source_rows]]
    reshape x2 -> x7, local copies, waits for them, and re-layouts: 1.25 us -> 5.2 us  [the longest x1 1.28 us: on_device(): blend_source.T.reshape(1, entries)]
  transfers between devices with their start and end apart: 3 -> 4, of which waited for: 3 -> 4; matrix products, arithmetic and copies ran while one was open for 1% -> 2% of each run, Pallas kernels for 0% -> 0%
where the time goes in v2:
time: 104 us; the launch traced here: 103 us
  waiting for transfers between devices  49.6 us (48%)
  starting transfers between devices  20.8 us (20%)
  Pallas kernels  16.3 us (16%)
  local copies, waits for them, and re-layouts  10.1 us (10%)
  matrix products  2.63 us (3%)
  other arithmetic  2.27 us (2%)
  between operations  1.43 us (1%)
    all_to_all x2, waiting for transfers between devices, exchange(): moved = lax.all_to_all(wire, 'dev', split_axis=0, concat_axis=0, tiled=True)  36 us
    pallas_call x1, Pallas kernels, on_device(): pl.pallas_call(functools.partial(fit_kernel, units=units), grid=(groups /...  14.8 us
    all_to_all x2, starting transfers between devices, exchange(): moved = lax.all_to_all(wire, 'dev', split_axis=0, concat_axis=0, tiled=True)  8.51 us
    all_to_all x1, starting transfers between devices, on_device(): lax.all_to_all(asking, 'dev', split_axis=0, concat_axis=0, tiled=True)  8.34 us
    all_to_all x1, waiting for transfers between devices, on_device(): lax.all_to_all(asking, 'dev', split_axis=0, concat_axis=0, tiled=True)  7.22 us
    all_to_all x1, waiting for transfers between devices, on_device(): lax.all_to_all(partial, ('grp', 'dev'), split_axis=0, concat_axis=0, tile...  6.33 us
    all_to_all x1, starting transfers between devices, on_device(): lax.all_to_all(partial, ('grp', 'dev'), split_axis=0, concat_axis=0, tile...  3.94 us
    transpose x1, local copies, waits for them, and re-layouts, exchange(): tiles.reshape(bands, peer_count, capacity, pixels).transpose(1, 2, 0, 3)  2.11 us
  transfers between devices with their start and end apart: 4, of which 4 were waited for; matrix products, arithmetic and copies ran while one was open for 2% of the time, Pallas kernels for 0%

profile of v2, /device:TPU:0, one launch (start us, length us, event | category | flops | bytes accessed | tf_op | source)
XLA Modules:
  0.0 103.2 jit_solution(10704757123202138284)
XLA Ops:
  0.6 1.3 %reshape.42.source_ref = s32[1,128]{1,0:T(1,128)} reshape(s32[2,64]{1,0:T(2,128)} %bitcast.53) | data formatting | bytes 1024 | tf_op jit(solution)/shard_map/reshape | solution.py:181
  1.9 1.3 %reshape.43.slot_ref = s32[1,128]{1,0:T(1,128)} reshape(s32[2,64]{1,0:T(2,128)} %bitcast.54) | data formatting | bytes 1024 | tf_op jit(solution)/shard_map/reshape | solution.py:181
  3.2 1.5 %place.1 = (s32[16,8]{1,0:T(8,128)}, s32[1,128]{1,0:T(1,128)}) custom-call(s32[1,128]{1,0:T(1,128)} %reshape.42.source_ref, s32[1,128]{1,0:T(1,128)} %reshape.43.slot_ref), custom_call_target="tpu_custom_call" | custom-call | tf_op jit(solution)/shard_map/place/pallas_call | solution.py:174
  4.7 8.3 %all-to-all-start = ((s32[16,1,8]{2,1,0:T(1,128)}), s32[16,1,8]{2,1,0:T(1,128)S(1)}, u32[]{:S(2)}, u32[]{:S(2)}) async-start(s32[16,1,8]{2,1,0:T(1,128)} %bitcast.52), calls=%async_computation | async-start | bytes 16384 | tf_op jit(solution)/shard_map/all_to_all | solution.py:182
  13.0 7.2 %all-to-all-done = s32[16,1,8]{2,1,0:T(1,128)S(1)} async-done(((s32[16,1,8]{2,1,0:T(1,128)}), s32[16,1,8]{2,1,0:T(1,128)S(1)}, u32[]{:S(2)}, u32[]{:S(2)}) %all-to-all-start) | async-done | bytes 544 | tf_op jit(solution)/shard_map/all_to_all | solution.py:182
  20.3 0.5 broadcast.7
  20.8 0.7 reduce.4
  21.5 1.6 %fusion = bf16[6,16,8,512]{3,2,1,0:T(8,128)(2,1)S(1)} fusion(f32[64,6,512]{2,0,1:T(8,128)} %param.6, s32[128]{0:T(128)S(1)} %eq.15, s32[64]{0:T(128)S(1)} %iota_add_fusion), kind=kOutput, calls=%fused_computation.2 | convolution fusion | flops 50929664 | bytes 1573632 | tf_op jit(solution)/shard_map/ts,tbp->bsp/dot_general | solution.py:186
  23.2 1.0 copy.71
  24.1 3.6 %all-to-all-start.1 = ((bf16[16,8,6,512]{3,1,2,0:T(8,128)(2,1)}), bf16[16,8,6,512]{3,1,2,0:T(8,128)(2,1)S(1)}, u32[]{:S(2)}, u32[]{:S(2)}) async-start(bf16[16,8,6,512]{3,1,2,0:T(8,128)(2,1)} %bitcast.51), calls=%async_computation.1 | async-start | bytes 1572864 | tf_op jit(solution)/shard_map/all_to_all | solution.py:192
  27.9 0.7 copy.50.sed_ref
  28.6 17.6 %all-to-all-done.1 = bf16[16,8,6,512]{3,1,2,0:T(8,128)(2,1)S(1)} async-done(((bf16[16,8,6,512]{3,1,2,0:T(8,128)(2,1)}), bf16[16,8,6,512]{3,1,2,0:T(8,128)(2,1)S(1)}, u32[]{:S(2)}, u32[]{:S(2)}) %all-to-all-start.1) | async-done | bytes 786464 | tf_op jit(solution)/shard_map/all_to_all | solution.py:192
  46.2 0.9 copy_bitcast_fusion.1.arrived_ref
  47.2 14.8 %fit.1 = (bf16[8,24,48]{2,1,0:T(8,128)(2,1)}, bf16[6,128,512]{2,1,0:T(8,128)(2,1)}) custom-call(s32[64]{0:T(128)} %count_ref.1, s32[1,128]{1,0:T(1,128)} %get-tuple-element.7.placing_ref, bf16[6,128,512]{2,1,0:T(8,128)(2,1)} %copy_bitcast_fusion.1.arrived_ref, bf16[8,24,48]{2,1,0:T(8,128)(2,1)} %copy.50.sed_ref, bf16[64,2,24,512]{3,2,1,0:T(8,128)(2,1)} %morph_ref.1), custom_call_target="tpu_custom_call" | custom-call | tf_op jit(solution)/shard_map/fit/pallas_call | solution.py:205
  62.0 2.1 %copy_bitcast_fusion = bf16[16,8,6,512]{3,1,2,0:T(8,128)(2,1)} fusion(bf16[6,128,512]{2,1,0:T(8,128)(2,1)} %get-tuple-element.8), kind=kLoop, calls=%fused_computation.5 | loop fusion | bytes 1572864 | tf_op jit(solution)/shard_map/transpose | solution.py:191
  64.1 4.9 %all-to-all-start.2 = ((bf16[16,8,6,512]{3,1,2,0:T(8,128)(2,1)}), bf16[16,8,6,512]{3,1,2,0:T(8,128)(2,1)S(1)}, u32[]{:S(2)}, u32[]{:S(2)}) async-start(bf16[16,8,6,512]{3,1,2,0:T(8,128)(2,1)} %copy_bitcast_fusion), calls=%async_computation.2 | async-start | bytes 1572864 | tf_op jit(solution)/shard_map/all_to_all | solution.py:192
  69.2 18.4 %all-to-all-done.2 = bf16[16,8,6,512]{3,1,2,0:T(8,128)(2,1)S(1)} async-done(((bf16[16,8,6,512]{3,1,2,0:T(8,128)(2,1)}), bf16[16,8,6,512]{3,1,2,0:T(8,128)(2,1)S(1)}, u32[]{:S(2)}, u32[]{:S(2)}) %all-to-all-start.2) | async-done | bytes 786464 | tf_op jit(solution)/shard_map/all_to_all | solution.py:192
  87.6 1.0 multiply_reduce_fusion
  88.6 1.3 %broadcast_in_dim.4 = f32[32,1,128]{2,1,0:T(1,128)} broadcast(f32[]{:T(128)} %get-tuple-element.18), dimensions={} | broadcast | bytes 16388 | tf_op jit(solution)/shard_map/broadcast_in_dim | solution.py:241
  89.8 3.9 %all-to-all-start.3 = ((f32[32,1,128]{2,1,0:T(1,128)}), f32[32,1,128]{2,1,0:T(1,128)S(1)}, u32[]{:S(2)}, u32[]{:S(2)}) async-start(f32[32,1,128]{2,1,0:T(1,128)} %broadcast_in_dim.4), calls=%async_computation.3 | async-start | bytes 32768 | tf_op jit(solution)/shard_map/all_to_all | solution.py:242
  93.8 0.7 copy.56
  94.5 6.3 %all-to-all-done.3 = f32[32,1,128]{2,1,0:T(1,128)S(1)} async-done(((f32[32,1,128]{2,1,0:T(1,128)}), f32[32,1,128]{2,1,0:T(1,128)S(1)}, u32[]{:S(2)}, u32[]{:S(2)}) %all-to-all-start.3) | async-done | bytes 16416 | tf_op jit(solution)/shard_map/all_to_all | solution.py:242
  100.9 0.6 slice_reduce_fusion
  102.2 1.0 broadcast_divide_fusion
  (12 shorter events, 0.4 us)
Async XLA Ops:
  0.6 27.1 %copy-start.2 = (bf16[64,24,6]{0,1,2:T(8,128)(2,1)S(1)}, bf16[64,24,6]{0,1,2:T(8,128)(2,1)}, u32[]{:S(2)}) copy-start(bf16[64,24,6]{0,1,2:T(8,128)(2,1)} %param.10) | copy-start | bytes 55300
  4.7 15.6 %all-to-all-start = ((s32[16,1,8]{2,1,0:T(1,128)}), s32[16,1,8]{2,1,0:T(1,128)S(1)}, u32[]{:S(2)}, u32[]{:S(2)}) async-start(s32[16,1,8]{2,1,0:T(1,128)} %bitcast.52), calls=%async_computation | async-start | bytes 16384 | tf_op jit(solution)/shard_map/all_to_all | solution.py:182
  24.1 22.1 %all-to-all-start.1 = ((bf16[16,8,6,512]{3,1,2,0:T(8,128)(2,1)}), bf16[16,8,6,512]{3,1,2,0:T(8,128)(2,1)S(1)}, u32[]{:S(2)}, u32[]{:S(2)}) async-start(bf16[16,8,6,512]{3,1,2,0:T(8,128)(2,1)} %bitcast.51), calls=%async_computation.1 | async-start | bytes 1572864 | tf_op jit(solution)/shard_map/all_to_all | solution.py:192
  47.2 40.4 %copy-start = (f32[64,6,512]{2,0,1:T(8,128)S(1)}, f32[64,6,512]{2,0,1:T(8,128)}, u32[]{:S(2)}) copy-start(f32[64,6,512]{2,0,1:T(8,128)} %param.6) | copy-start | bytes 2359300
  62.0 7.0 %copy-start.1 = (bf16[8,24,48]{2,1,0:T(8,128)(2,1)S(1)}, bf16[8,24,48]{2,1,0:T(8,128)(2,1)}, u32[]{:S(2)}) copy-start(bf16[8,24,48]{2,1,0:T(8,128)(2,1)} %get-tuple-element.9) | copy-start | bytes 55300
  64.1 23.4 %all-to-all-start.2 = ((bf16[16,8,6,512]{3,1,2,0:T(8,128)(2,1)}), bf16[16,8,6,512]{3,1,2,0:T(8,128)(2,1)S(1)}, u32[]{:S(2)}, u32[]{:S(2)}) async-start(bf16[16,8,6,512]{3,1,2,0:T(8,128)(2,1)} %copy_bitcast_fusion), calls=%async_computation.2 | async-start | bytes 1572864 | tf_op jit(solution)/shard_map/all_to_all | solution.py:192
  89.8 11.0 %all-to-all-start.3 = ((f32[32,1,128]{2,1,0:T(1,128)}), f32[32,1,128]{2,1,0:T(1,128)S(1)}, u32[]{:S(2)}, u32[]{:S(2)}) async-start(f32[32,1,128]{2,1,0:T(1,128)} %broadcast_in_dim.4), calls=%async_computation.3 | async-start | bytes 32768 | tf_op jit(solution)/shard_map/all_to_all | solution.py:242

commit v3 on v2

--- a/solution.py
+++ b/solution.py
@@ -36,18 +36,72 @@
 
 def place_kernel(source_ref, slot_ref, asking_ref, placing_ref):
     peers, capacity = asking_ref.shape
-    entries = source_ref.shape[1]
+    footprint, blends = source_ref.shape
+    entries = footprint * blends
+    source = jnp.concatenate([source_ref[f : f + 1, :] for f in range(footprint)], axis=1)
+    slot = jnp.concatenate([slot_ref[f : f + 1, :] for f in range(footprint)], axis=1)
     peer = lax.broadcasted_iota(jnp.int32, (peers, entries), 0)
-    named = peer == source_ref[...]
+    named = peer == source
     before = lax.broadcasted_iota(jnp.int32, (entries, entries), 0)
     after = lax.broadcasted_iota(jnp.int32, (entries, entries), 1)
     upto = (before <= after).astype(F32).astype(BF16)
     rank = dot(named.astype(F32).astype(BF16), upto, 1, 0).astype(jnp.int32) - 1
     placing_ref[...] = jnp.sum(jnp.where(named, peer * capacity + rank, 0), axis=0, keepdims=True)
-    value = jnp.broadcast_to(slot_ref[...] + 1, (peers, entries))
+    value = jnp.broadcast_to(slot + 1, (peers, entries))
     for s in range(capacity):
         hit = jnp.where(named & (rank == s), value, 0)
         asking_ref[:, s : s + 1] = jnp.sum(hit, axis=1, keepdims=True)
+
+
+def read_band(ref, b):
+    if len(ref.shape) == 3:
+        return ref[b]
+    peers, _, capacity, pixels = ref.shape
+    return ref[:, b].astype(F32).reshape(peers * capacity, pixels).astype(BF16)
+
+
+def write_band(ref, b, value):
+    if len(ref.shape) == 3:
+        ref[b] = value.astype(BF16)
+    else:
+        peers, _, capacity, pixels = ref.shape
+        ref[:, b] = value.reshape(peers, capacity, pixels).astype(BF16)
+
+
+def send_kernel(wanted_ref, tiles_ref, selector_ref, out_ref):
+    peers, capacity = wanted_ref.shape
+    bands, tile_rows, _ = tiles_ref.shape
+    slots = peers * capacity
+    lane = lax.broadcasted_iota(jnp.int32, (capacity, slots), 1)
+    within = lax.broadcasted_iota(jnp.int32, (capacity, slots), 0)
+    spread = (lane % capacity == within).astype(F32)
+    wide = lax.dot_general(
+        wanted_ref[...].astype(F32), spread, (((1,), (0,)), ((), ())),
+        precision=lax.Precision.HIGHEST, preferred_element_type=F32,
+    )
+    peer = lax.broadcasted_iota(jnp.int32, (peers, slots), 0)
+    column = lax.broadcasted_iota(jnp.int32, (peers, slots), 1)
+    mine = (column >= peer * capacity) & (column < (peer + 1) * capacity)
+    wanted = jnp.sum(jnp.where(mine, wide, 0.0), axis=0, keepdims=True).astype(jnp.int32)
+    tile = lax.broadcasted_iota(jnp.int32, (tile_rows, slots), 0) + 1
+    selector = (tile == wanted).astype(F32).astype(BF16)
+    selector_ref[...] = selector
+    for b in range(bands):
+        write_band(out_ref, b, dot(selector, tiles_ref[b].astype(BF16), 0, 0))
+
+
+def residual_kernel(selector_ref, tiles_ref, returned_ref, residual_ref, partial_ref):
+    bands = tiles_ref.shape[0]
+    selector = selector_ref[...]
+    squares = jnp.zeros(tiles_ref.shape[1:], F32)
+    for b in range(bands):
+        residual = tiles_ref[b] - dot(selector, read_band(returned_ref, b), 1, 0)
+        residual_ref[b] = residual
+        squares = squares + residual * residual
+    partial_ref[...] = jnp.broadcast_to(
+        jnp.sum(jnp.sum(squares, axis=0, keepdims=True), axis=1, keepdims=True)[None],
+        partial_ref.shape,
+    )
 
 
 def fit_kernel(
@@ -55,8 +109,8 @@
     x_ref, mask_ref, data_ref, model_ref, *, units,
 ):
     step = pl.program_id(0)
-    bands, slots, pixels = arrived_ref.shape
-    entries = placing_ref.shape[1]
+    bands, entries, pixels = data_ref.shape
+    slots = math.prod(arrived_ref.shape) // (bands * pixels)
     footprint, components = morph_ref.shape[1:3]
     blends = entries // footprint
     rows = LANES * components
@@ -71,7 +125,7 @@
     def _():
         chosen = permutation()
         for b in range(bands):
-            data_ref[b] = dot(chosen, arrived_ref[b], 0, 0)
+            data_ref[b] = dot(chosen, read_band(arrived_ref, b), 0, 0)
         lane = lax.broadcasted_iota(jnp.int32, (components, depth), 1)
         for n in range(LANES):
             own = (lane >= components * n) & (lane < components * (n + 1))
@@ -160,7 +214,7 @@
     def _():
         chosen = permutation()
         for b in range(bands):
-            out_ref[b] = dot(chosen, model_ref[b].astype(BF16), 1, 0).astype(BF16)
+            write_band(out_ref, b, dot(chosen, model_ref[b].astype(BF16), 1, 0))
 
 
 def on_device(pixel_tiles, blend_source, blend_slot, component_count, sed_start, morph_start):
@@ -177,20 +231,29 @@
             jax.ShapeDtypeStruct((peer_count, capacity), jnp.int32),
             jax.ShapeDtypeStruct((1, entries), jnp.int32),
         ),
+        compiler_params=pltpu.CompilerParams(vmem_limit_bytes=16 * 2**20),
         name="place",
-    )(blend_source.T.reshape(1, entries), blend_slot.T.reshape(1, entries))
-    wanted = lax.all_to_all(asking, "dev", split_axis=0, concat_axis=0, tiled=True).reshape(slots)
-    selector = (
-        wanted[None, :] == jnp.arange(1, tile_rows + 1, dtype=jnp.int32)[:, None]
-    ).astype(BF16)
-    outgoing = jnp.einsum(
-        "ts,tbp->bsp", selector, pixel_tiles.astype(BF16), preferred_element_type=F32
-    ).astype(BF16)
-
-    def exchange(tiles):
-        wire = tiles.reshape(bands, peer_count, capacity, pixels).transpose(1, 2, 0, 3)
+    )(blend_source.T, blend_slot.T)
+    wanted = lax.all_to_all(asking, "dev", split_axis=0, concat_axis=0, tiled=True)
+    direct = capacity % 8 == 0
+    banded = (bands, slots, pixels)
+    tile_shape = (peer_count, bands, capacity, pixels) if direct else banded
+    tiles = pixel_tiles.transpose(1, 0, 2)
+    selector, outgoing = pl.pallas_call(
+        send_kernel,
+        out_shape=(
+            jax.ShapeDtypeStruct((tile_rows, slots), BF16),
+            jax.ShapeDtypeStruct(tile_shape, BF16),
+        ),
+        compiler_params=pltpu.CompilerParams(vmem_limit_bytes=16 * 2**20),
+        name="send",
+    )(wanted, tiles)
+
+    def exchange(wire):
+        if not direct:
+            wire = wire.reshape(bands, peer_count, capacity, pixels).transpose(1, 2, 0, 3)
         moved = lax.all_to_all(wire, "dev", split_axis=0, concat_axis=0, tiled=True)
-        return moved.transpose(2, 0, 1, 3).reshape(bands, slots, pixels)
+        return moved if direct else moved.transpose(2, 0, 1, 3).reshape(banded)
 
     arrived = exchange(outgoing)
     groups = blend_rows // LANES
@@ -207,18 +270,18 @@
         grid=(groups // units,),
         in_specs=[
             pl.BlockSpec(memory_space=pltpu.SMEM),
-            pl.BlockSpec((1, entries), lambda i: (0, 0)),
-            pl.BlockSpec((bands, slots, pixels), lambda i: (0, 0, 0)),
+            pl.BlockSpec(memory_space=pltpu.VMEM),
+            pl.BlockSpec(memory_space=pltpu.VMEM),
             pl.BlockSpec((units, components, cols), lambda i: (i, 0, 0)),
             pl.BlockSpec((units * LANES, footprint, components, pixels), lambda i: (i, 0, 0, 0)),
         ],
         out_specs=[
             pl.BlockSpec((units, components, cols), lambda i: (i, 0, 0)),
-            pl.BlockSpec((bands, slots, pixels), lambda i: (0, 0, 0)),
+            pl.BlockSpec(tile_shape, lambda i: (0,) * len(tile_shape)),
         ],
         out_shape=(
             jax.ShapeDtypeStruct((groups, components, cols), BF16),
-            jax.ShapeDtypeStruct((bands, slots, pixels), BF16),
+            jax.ShapeDtypeStruct(tile_shape, BF16),
         ),
         scratch_shapes=[
             pltpu.VMEM((units, depth, footprint * pixels), BF16),
@@ -226,7 +289,9 @@
             pltpu.VMEM((bands, entries, pixels), F32),
             pltpu.VMEM((bands, entries, pixels), F32),
         ],
-        compiler_params=pltpu.CompilerParams(dimension_semantics=("arbitrary",)),
+        compiler_params=pltpu.CompilerParams(
+            dimension_semantics=("arbitrary",), vmem_limit_bytes=24 * 2**20
+        ),
         name="fit",
     )(component_count, placing, arrived, sed_in, morph_start)
     sed_final = (
@@ -235,15 +300,23 @@
         .reshape(sed_start.shape)
     )
     returned = exchange(models)
-    summed = jnp.einsum("ts,bsp->tbp", selector, returned, preferred_element_type=F32)
-    residual = pixel_tiles - summed
     everyone = lax.axis_size("grp") * peer_count
-    partial = jnp.broadcast_to(jnp.sum(residual * residual), (everyone, 1, 128))
+    residual, partial = pl.pallas_call(
+        residual_kernel,
+        out_shape=(
+            jax.ShapeDtypeStruct((bands, tile_rows, pixels), F32),
+            jax.ShapeDtypeStruct((everyone, 1, 128), F32),
+        ),
+        in_specs=[pl.BlockSpec(memory_space=pltpu.VMEM)] * 3,
+        out_specs=[pl.BlockSpec(memory_space=pltpu.VMEM)] * 2,
+        compiler_params=pltpu.CompilerParams(vmem_limit_bytes=16 * 2**20),
+        name="residual",
+    )(selector, tiles, returned)
     partials = lax.all_to_all(partial, ("grp", "dev"), split_axis=0, concat_axis=0, tiled=True)
     total_sq = jnp.sum(partials[:, 0, 0])
     pixel_count = float(residual.size * everyone)
     whitened = residual / jnp.sqrt(total_sq / pixel_count + 1e-06)
-    return (whitened, sed_final)
+    return (whitened.transpose(1, 0, 2), sed_final)
 
 
 def solution(mesh):

time: 104 us -> 97.1 us (0.934)
  blocking collectives: 0 us -> 15.4 us
  starting transfers between devices: 20.8 us -> 12.4 us
  waiting for transfers between devices: 49.6 us -> 42.2 us
  local copies, waits for them, and re-layouts: 10.1 us -> 6.96 us
  matrix products: 2.63 us -> 0 us
    all_to_all x0 -> x1, blocking collectives: none -> 15.4 us  [on_device(): lax.all_to_all(asking, 'dev', split_axis=0, concat_axis=0, tiled=True)]
    all_to_all x1 -> x0, starting transfers between devices: 8.34 us -> none  [on_device(): lax.all_to_all(asking, 'dev', split_axis=0, concat_axis=0, tiled=True)]
    all_to_all x1 -> x0, waiting for transfers between devices: 7.22 us -> none  [on_device(): lax.all_to_all(asking, 'dev', split_axis=0, concat_axis=0, tiled=True)]
    unnamed x8 -> x14, local copies, waits for them, and re-layouts: 0.85 us -> 6.71 us
    reshape x4 -> x0, local copies, waits for them, and re-layouts: 4.45 us -> none  [the longest x1 1.28 us: on_device(): blend_source.T.reshape(1, entries)]
    dot_general x2 -> x0, matrix products: 2.63 us -> none  [the longest x1 1.62 us: on_device(): jnp.einsum('ts,tbp->bsp', selector, pixel_tiles.astype(BF16), preferred_e...]
    pallas_call x0 -> x2, Pallas kernels: none -> 2.39 us  [the longest x1 1.42 us: on_device(): pl.pallas_call(send_kernel, out_shape=(jax.ShapeDtypeStruct((tile_rows, s...]
    transpose x1 -> x0, local copies, waits for them, and re-layouts: 2.11 us -> none  [exchange(): tiles.reshape(bands, peer_count, capacity, pixels).transpose(1, 2, 0, 3)]
  transfers between devices with their start and end apart: 4 -> 3, of which waited for: 4 -> 3; matrix products, arithmetic and copies ran while one was open for 2% -> 2% of each run, Pallas kernels for 0% -> 0%
where the time goes in v3:
time: 97.1 us; the launch traced here: 96.5 us
  waiting for transfers between devices  42.2 us (43%)
  Pallas kernels  16.5 us (17%)
  blocking collectives  15.4 us (16%)
  starting transfers between devices  12.4 us (13%)
  local copies, waits for them, and re-layouts  6.96 us (7%)
  other arithmetic  1.6 us (2%)
  between operations  1.41 us (1%)
    all_to_all x2, waiting for transfers between devices, exchange(): moved = lax.all_to_all(wire, 'dev', split_axis=0, concat_axis=0, tiled=True)  35.8 us
    all_to_all x1, blocking collectives, on_device(): lax.all_to_all(asking, 'dev', split_axis=0, concat_axis=0, tiled=True)  15.4 us
    pallas_call x1, Pallas kernels, on_device(): pl.pallas_call(functools.partial(fit_kernel, units=units), grid=(groups /...  13.8 us
    all_to_all x2, starting transfers between devices, exchange(): moved = lax.all_to_all(wire, 'dev', split_axis=0, concat_axis=0, tiled=True)  8.51 us
    unnamed x14, local copies, waits for them, and re-layouts  6.71 us
    all_to_all x1, waiting for transfers between devices, on_device(): lax.all_to_all(partial, ('grp', 'dev'), split_axis=0, concat_axis=0, tile...  6.33 us
    all_to_all x1, starting transfers between devices, on_device(): lax.all_to_all(partial, ('grp', 'dev'), split_axis=0, concat_axis=0, tile...  3.93 us
  transfers between devices with their start and end apart: 3, of which 3 were waited for; matrix products, arithmetic and copies ran while one was open for 2% of the time, Pallas kernels for 0%

profile of v3, /device:TPU:0, one launch (start us, length us, event | category | flops | bytes accessed | tf_op | source)
XLA Modules:
  0.0 96.5 jit_solution(13086871685064062178)
XLA Ops:
  0.6 0.7 copy-done.3
  1.3 0.7 copy-done.4
  2.0 0.3 place.1
  2.3 15.4 %all_to_all.26 = s32[16,1,8]{2,1,0:T(1,128)S(1)} all-to-all(s32[16,1,8]{2,1,0:T(1,128)S(1)} %bitcast.26), channel_id=1, replica_groups=mesh['grp'=2,'dev'=16] {'dev'}, dimensions={0} | all-to-all | bytes 1024 | tf_op jit(solution)/shard_map/all_to_all | solution.py:237
  17.7 1.1 %copy-done = f32[64,6,512]{2,0,1:T(8,128)S(1)} copy-done((f32[64,6,512]{2,0,1:T(8,128)S(1)}, f32[64,6,512]{2,0,1:T(8,128)}, u32[]{:S(2)}) %copy-start) | copy-done | bytes 786456
  18.9 1.4 %send.1 = (bf16[64,128]{1,0:T(8,128)(2,1)S(1)}, bf16[16,6,8,512]{3,2,1,0:T(8,128)(2,1)}) custom-call(s32[16,8]{1,0:T(8,128)S(1)} %bitcast.25, f32[6,64,512]{2,1,0:T(8,128)S(1)} %bitcast.23), custom_call_target="tpu_custom_call" | custom-call | tf_op jit(solution)/shard_map/send/pallas_call | solution.py:242
  20.3 3.6 %all-to-all-start.1 = ((bf16[16,6,8,512]{3,2,1,0:T(8,128)(2,1)}), bf16[16,6,8,512]{3,2,1,0:T(8,128)(2,1)S(1)}, u32[]{:S(2)}, u32[]{:S(2)}) async-start(bf16[16,6,8,512]{3,2,1,0:T(8,128)(2,1)} %get-tuple-element.13), calls=%async_computation.1 | async-start | bytes 1572864 | tf_op jit(solution)/shard_map/all_to_all | solution.py:255
  23.9 0.0 copy-start.1
  23.9 1.0 copy.24
  24.9 0.1 copy.26.sed_ref
  25.0 17.4 %all-to-all-done.1.arrived_ref = bf16[16,6,8,512]{3,2,1,0:T(8,128)(2,1)S(1)} async-done(((bf16[16,6,8,512]{3,2,1,0:T(8,128)(2,1)}), bf16[16,6,8,512]{3,2,1,0:T(8,128)(2,1)S(1)}, u32[]{:S(2)}, u32[]{:S(2)}) %all-to-all-start.1) | async-done | bytes 786464 | tf_op jit(solution)/shard_map/all_to_all | solution.py:255
  42.4 1.9 %copy-done.2 = bf16[64,2,24,512]{3,2,1,0:T(8,128)(2,1)S(1)} copy-done((bf16[64,2,24,512]{3,2,1,0:T(8,128)(2,1)S(1)}, bf16[64,2,24,512]{3,2,1,0:T(8,128)(2,1)}, u32[]{:S(2)}) %copy-start.2) | copy-done | bytes 3145752
  44.3 0.7 copy-done.5
  45.0 13.8 %fit.1 = (bf16[8,24,48]{2,1,0:T(8,128)(2,1)S(1)}, bf16[16,6,8,512]{3,2,1,0:T(8,128)(2,1)}) custom-call(s32[64]{0:T(128)S(1)} %copy-done.5, s32[1,128]{1,0:T(1,128)S(1)} %get-tuple-element.12.placing_ref, bf16[16,6,8,512]{3,2,1,0:T(8,128)(2,1)S(1)} %all-to-all-done.1.arrived_ref, bf16[8,24,48]{2,1,0:T(8,128)(2,1)S(1)} %copy.26.sed_ref, ...), custom_call_target="tpu_custom_call" | custom-call | tf_op jit(solution)/shard_map/fit/pallas_call | solution.py:268
  58.8 4.9 %all-to-all-start.2 = ((bf16[16,6,8,512]{3,2,1,0:T(8,128)(2,1)}), bf16[16,6,8,512]{3,2,1,0:T(8,128)(2,1)S(1)}, u32[]{:S(2)}, u32[]{:S(2)}) async-start(bf16[16,6,8,512]{3,2,1,0:T(8,128)(2,1)} %get-tuple-element.14), calls=%async_computation.2 | async-start | bytes 1572864 | tf_op jit(solution)/shard_map/all_to_all | solution.py:255
  63.7 0.1 copy.27
  63.8 18.4 %all-to-all-done.2.returned_ref = bf16[16,6,8,512]{3,2,1,0:T(8,128)(2,1)S(1)} async-done(((bf16[16,6,8,512]{3,2,1,0:T(8,128)(2,1)}), bf16[16,6,8,512]{3,2,1,0:T(8,128)(2,1)S(1)}, u32[]{:S(2)}, u32[]{:S(2)}) %all-to-all-start.2) | async-done | bytes 786464 | tf_op jit(solution)/shard_map/all_to_all | solution.py:255
  82.2 0.0 copy-done.1
  82.3 1.0 %residual.1 = (f32[6,64,512]{2,1,0:T(8,128)S(1)}, f32[32,1,128]{2,1,0:T(1,128)}) custom-call(bf16[64,128]{1,0:T(8,128)(2,1)S(1)} %get-tuple-element.11.selector_ref, f32[6,64,512]{2,1,0:T(8,128)S(1)} %bitcast.24, bf16[16,6,8,512]{3,2,1,0:T(8,128)(2,1)S(1)} %all-to-all-done.2.returned_ref), custom_call_target="tpu_custom_call" | custom-call | tf_op jit(solution)/shard_map/residual/pallas_call | solution.py:304
  83.2 3.9 %all-to-all-start.3 = ((f32[32,1,128]{2,1,0:T(1,128)}), f32[32,1,128]{2,1,0:T(1,128)S(1)}, u32[]{:S(2)}, u32[]{:S(2)}) async-start(f32[32,1,128]{2,1,0:T(1,128)} %get-tuple-element.16), calls=%async_computation.3 | async-start | bytes 32768 | tf_op jit(solution)/shard_map/all_to_all | solution.py:315
  87.2 0.7 copy.29
  87.9 6.3 %all-to-all-done.3 = f32[32,1,128]{2,1,0:T(1,128)S(1)} async-done(((f32[32,1,128]{2,1,0:T(1,128)}), f32[32,1,128]{2,1,0:T(1,128)S(1)}, u32[]{:S(2)}, u32[]{:S(2)}) %all-to-all-start.3) | async-done | bytes 16416 | tf_op jit(solution)/shard_map/all_to_all | solution.py:315
  94.2 0.6 slice_reduce_fusion
  95.6 1.0 %divide_bitcast_fusion = f32[64,6,512]{2,0,1:T(8,128)} fusion(f32[6,64,512]{2,1,0:T(8,128)S(1)} %get-tuple-element.15, f32[]{:T(128)S(6)} %sqrt.3), kind=kLoop, calls=%fused_computation | loop fusion | flops 196608 | bytes 1572868 | tf_op jit(solution)/shard_map/transpose | solution.py:319
  (7 shorter events, 0.0 us)
Async XLA Ops:
  0.6 0.7 copy-start.3
  1.3 0.7 copy-start.4
  17.7 1.1 %copy-start = (f32[64,6,512]{2,0,1:T(8,128)S(1)}, f32[64,6,512]{2,0,1:T(8,128)}, u32[]{:S(2)}) copy-start(f32[64,6,512]{2,0,1:T(8,128)} %param.6) | copy-start | bytes 2359300
  20.3 22.1 %all-to-all-start.1 = ((bf16[16,6,8,512]{3,2,1,0:T(8,128)(2,1)}), bf16[16,6,8,512]{3,2,1,0:T(8,128)(2,1)S(1)}, u32[]{:S(2)}, u32[]{:S(2)}) async-start(bf16[16,6,8,512]{3,2,1,0:T(8,128)(2,1)} %get-tuple-element.13), calls=%async_computation.1 | async-start | bytes 1572864 | tf_op jit(solution)/shard_map/all_to_all | solution.py:255
  23.9 58.3 %copy-start.1 = (f32[64,6,512]{2,0,1:T(8,128)S(1)}, f32[64,6,512]{2,0,1:T(8,128)}, u32[]{:S(2)}) copy-start(f32[64,6,512]{2,0,1:T(8,128)} %param.6) | copy-start | bytes 2359300
  42.4 1.9 %copy-start.2 = (bf16[64,2,24,512]{3,2,1,0:T(8,128)(2,1)S(1)}, bf16[64,2,24,512]{3,2,1,0:T(8,128)(2,1)}, u32[]{:S(2)}) copy-start(bf16[64,2,24,512]{3,2,1,0:T(8,128)(2,1)} %morph_ref.1) | copy-start | bytes 9437188
  44.3 0.7 copy-start.5
  58.8 23.5 %all-to-all-start.2 = ((bf16[16,6,8,512]{3,2,1,0:T(8,128)(2,1)}), bf16[16,6,8,512]{3,2,1,0:T(8,128)(2,1)S(1)}, u32[]{:S(2)}, u32[]{:S(2)}) async-start(bf16[16,6,8,512]{3,2,1,0:T(8,128)(2,1)} %get-tuple-element.14), calls=%async_computation.2 | async-start | bytes 1572864 | tf_op jit(solution)/shard_map/all_to_all | solution.py:255
  83.2 11.0 %all-to-all-start.3 = ((f32[32,1,128]{2,1,0:T(1,128)}), f32[32,1,128]{2,1,0:T(1,128)S(1)}, u32[]{:S(2)}, u32[]{:S(2)}) async-start(f32[32,1,128]{2,1,0:T(1,128)} %get-tuple-element.16), calls=%async_computation.3 | async-start | bytes 32768 | tf_op jit(solution)/shard_map/all_to_all | solution.py:315

commit v4 on v3

--- a/solution.py
+++ b/solution.py
@@ -257,7 +257,7 @@
 
     arrived = exchange(outgoing)
     groups = blend_rows // LANES
-    units = math.gcd(groups, 2)
+    units = math.gcd(groups, 4)
     rows, cols = LANES * components, LANES * bands
     depth = -(-(rows + cols) // 128) * 128
     sed_in = (

time: 97.1 us -> 95 us (0.978)
  Pallas kernels: 16.5 us -> 14.4 us
    pallas_call x1, Pallas kernels: 13.8 us -> 11.7 us  [on_device(): pl.pallas_call(functools.partial(fit_kernel, units=units), grid=(groups /...]
where the time goes in v4:
time: 95 us; the launch traced here: 94.5 us
  waiting for transfers between devices  42.2 us (44%)
  blocking collectives  15.4 us (16%)
  Pallas kernels  14.4 us (15%)
  starting transfers between devices  12.4 us (13%)
  local copies, waits for them, and re-layouts  6.96 us (7%)
  other arithmetic  1.6 us (2%)
  between operations  1.41 us (1%)
    all_to_all x2, waiting for transfers between devices, exchange(): moved = lax.all_to_all(wire, 'dev', split_axis=0, concat_axis=0, tiled=True)  35.8 us
    all_to_all x1, blocking collectives, on_device(): lax.all_to_all(asking, 'dev', split_axis=0, concat_axis=0, tiled=True)  15.4 us
    pallas_call x1, Pallas kernels, on_device(): pl.pallas_call(functools.partial(fit_kernel, units=units), grid=(groups /...  11.7 us
    all_to_all x2, starting transfers between devices, exchange(): moved = lax.all_to_all(wire, 'dev', split_axis=0, concat_axis=0, tiled=True)  8.51 us
    unnamed x14, local copies, waits for them, and re-layouts  6.71 us
    all_to_all x1, waiting for transfers between devices, on_device(): lax.all_to_all(partial, ('grp', 'dev'), split_axis=0, concat_axis=0, tile...  6.33 us
    all_to_all x1, starting transfers between devices, on_device(): lax.all_to_all(partial, ('grp', 'dev'), split_axis=0, concat_axis=0, tile...  3.94 us
  transfers between devices with their start and end apart: 3, of which 3 were waited for; matrix products, arithmetic and copies ran while one was open for 2% of the time, Pallas kernels for 0%

profile of v4, /device:TPU:0, one launch (start us, length us, event | category | flops | bytes accessed | tf_op | source)
XLA Modules:
  0.0 94.5 jit_solution(9494745154055691745)
XLA Ops:
  0.6 0.0 copy-start.3
  0.6 0.7 copy-done.3
  1.3 0.7 copy-done.4
  2.0 0.3 place.1
  2.3 15.4 %all_to_all.26 = s32[16,1,8]{2,1,0:T(1,128)S(1)} all-to-all(s32[16,1,8]{2,1,0:T(1,128)S(1)} %bitcast.26), channel_id=1, replica_groups=mesh['grp'=2,'dev'=16] {'dev'}, dimensions={0} | all-to-all | bytes 1024 | tf_op jit(solution)/shard_map/all_to_all | solution.py:237
  17.7 1.1 %copy-done = f32[64,6,512]{2,0,1:T(8,128)S(1)} copy-done((f32[64,6,512]{2,0,1:T(8,128)S(1)}, f32[64,6,512]{2,0,1:T(8,128)}, u32[]{:S(2)}) %copy-start) | copy-done | bytes 786456
  18.9 1.4 %send.1 = (bf16[64,128]{1,0:T(8,128)(2,1)S(1)}, bf16[16,6,8,512]{3,2,1,0:T(8,128)(2,1)}) custom-call(s32[16,8]{1,0:T(8,128)S(1)} %bitcast.25, f32[6,64,512]{2,1,0:T(8,128)S(1)} %bitcast.23), custom_call_target="tpu_custom_call" | custom-call | tf_op jit(solution)/shard_map/send/pallas_call | solution.py:242
  20.3 3.6 %all-to-all-start.1 = ((bf16[16,6,8,512]{3,2,1,0:T(8,128)(2,1)}), bf16[16,6,8,512]{3,2,1,0:T(8,128)(2,1)S(1)}, u32[]{:S(2)}, u32[]{:S(2)}) async-start(bf16[16,6,8,512]{3,2,1,0:T(8,128)(2,1)} %get-tuple-element.13), calls=%async_computation.1 | async-start | bytes 1572864 | tf_op jit(solution)/shard_map/all_to_all | solution.py:255
  23.9 0.0 copy-start.1
  23.9 1.0 %copy.24 = bf16[64,24,6]{1,0,2:T(8,128)(2,1)S(1)} copy(bf16[64,24,6]{0,1,2:T(8,128)(2,1)} %param.10) | data formatting | bytes 36864 | tf_op args[4]
  24.9 0.1 copy.26.sed_ref
  25.0 17.4 %all-to-all-done.1.arrived_ref = bf16[16,6,8,512]{3,2,1,0:T(8,128)(2,1)S(1)} async-done(((bf16[16,6,8,512]{3,2,1,0:T(8,128)(2,1)}), bf16[16,6,8,512]{3,2,1,0:T(8,128)(2,1)S(1)}, u32[]{:S(2)}, u32[]{:S(2)}) %all-to-all-start.1) | async-done | bytes 786464 | tf_op jit(solution)/shard_map/all_to_all | solution.py:255
  42.4 1.9 %copy-done.2 = bf16[64,2,24,512]{3,2,1,0:T(8,128)(2,1)S(1)} copy-done((bf16[64,2,24,512]{3,2,1,0:T(8,128)(2,1)S(1)}, bf16[64,2,24,512]{3,2,1,0:T(8,128)(2,1)}, u32[]{:S(2)}) %copy-start.2) | copy-done | bytes 3145752
  44.3 0.7 copy-done.5
  45.0 11.7 %fit.1 = (bf16[8,24,48]{2,1,0:T(8,128)(2,1)S(1)}, bf16[16,6,8,512]{3,2,1,0:T(8,128)(2,1)}) custom-call(s32[64]{0:T(128)S(1)} %copy-done.5, s32[1,128]{1,0:T(1,128)S(1)} %get-tuple-element.12.placing_ref, bf16[16,6,8,512]{3,2,1,0:T(8,128)(2,1)S(1)} %all-to-all-done.1.arrived_ref, bf16[8,24,48]{2,1,0:T(8,128)(2,1)S(1)} %copy.26.sed_ref, ...), custom_call_target="tpu_custom_call" | custom-call | tf_op jit(solution)/shard_map/fit/pallas_call | solution.py:268
  56.7 4.9 %all-to-all-start.2 = ((bf16[16,6,8,512]{3,2,1,0:T(8,128)(2,1)}), bf16[16,6,8,512]{3,2,1,0:T(8,128)(2,1)S(1)}, u32[]{:S(2)}, u32[]{:S(2)}) async-start(bf16[16,6,8,512]{3,2,1,0:T(8,128)(2,1)} %get-tuple-element.14), calls=%async_computation.2 | async-start | bytes 1572864 | tf_op jit(solution)/shard_map/all_to_all | solution.py:255
  61.6 0.1 copy.27
  61.8 18.4 %all-to-all-done.2.returned_ref = bf16[16,6,8,512]{3,2,1,0:T(8,128)(2,1)S(1)} async-done(((bf16[16,6,8,512]{3,2,1,0:T(8,128)(2,1)}), bf16[16,6,8,512]{3,2,1,0:T(8,128)(2,1)S(1)}, u32[]{:S(2)}, u32[]{:S(2)}) %all-to-all-start.2) | async-done | bytes 786464 | tf_op jit(solution)/shard_map/all_to_all | solution.py:255
  80.2 1.0 %residual.1 = (f32[6,64,512]{2,1,0:T(8,128)S(1)}, f32[32,1,128]{2,1,0:T(1,128)}) custom-call(bf16[64,128]{1,0:T(8,128)(2,1)S(1)} %get-tuple-element.11.selector_ref, f32[6,64,512]{2,1,0:T(8,128)S(1)} %bitcast.24, bf16[16,6,8,512]{3,2,1,0:T(8,128)(2,1)S(1)} %all-to-all-done.2.returned_ref), custom_call_target="tpu_custom_call" | custom-call | tf_op jit(solution)/shard_map/residual/pallas_call | solution.py:304
  81.2 3.9 %all-to-all-start.3 = ((f32[32,1,128]{2,1,0:T(1,128)}), f32[32,1,128]{2,1,0:T(1,128)S(1)}, u32[]{:S(2)}, u32[]{:S(2)}) async-start(f32[32,1,128]{2,1,0:T(1,128)} %get-tuple-element.16), calls=%async_computation.3 | async-start | bytes 32768 | tf_op jit(solution)/shard_map/all_to_all | solution.py:315
  85.1 0.7 copy.29
  85.8 6.3 %all-to-all-done.3 = f32[32,1,128]{2,1,0:T(1,128)S(1)} async-done(((f32[32,1,128]{2,1,0:T(1,128)}), f32[32,1,128]{2,1,0:T(1,128)S(1)}, u32[]{:S(2)}, u32[]{:S(2)}) %all-to-all-start.3) | async-done | bytes 16416 | tf_op jit(solution)/shard_map/all_to_all | solution.py:315
  92.2 0.6 slice_reduce_fusion
  93.5 1.0 %divide_bitcast_fusion = f32[64,6,512]{2,0,1:T(8,128)} fusion(f32[6,64,512]{2,1,0:T(8,128)S(1)} %get-tuple-element.15, f32[]{:T(128)S(6)} %sqrt.3), kind=kLoop, calls=%fused_computation | loop fusion | flops 196608 | bytes 1572868 | tf_op jit(solution)/shard_map/transpose | solution.py:319
  (7 shorter events, 0.0 us)
Async XLA Ops:
  0.6 0.7 copy-start.3
  1.3 0.7 copy-start.4
  17.7 1.1 %copy-start = (f32[64,6,512]{2,0,1:T(8,128)S(1)}, f32[64,6,512]{2,0,1:T(8,128)}, u32[]{:S(2)}) copy-start(f32[64,6,512]{2,0,1:T(8,128)} %param.6) | copy-start | bytes 2359300
  20.3 22.1 %all-to-all-start.1 = ((bf16[16,6,8,512]{3,2,1,0:T(8,128)(2,1)}), bf16[16,6,8,512]{3,2,1,0:T(8,128)(2,1)S(1)}, u32[]{:S(2)}, u32[]{:S(2)}) async-start(bf16[16,6,8,512]{3,2,1,0:T(8,128)(2,1)} %get-tuple-element.13), calls=%async_computation.1 | async-start | bytes 1572864 | tf_op jit(solution)/shard_map/all_to_all | solution.py:255
  23.9 56.3 %copy-start.1 = (f32[64,6,512]{2,0,1:T(8,128)S(1)}, f32[64,6,512]{2,0,1:T(8,128)}, u32[]{:S(2)}) copy-start(f32[64,6,512]{2,0,1:T(8,128)} %param.6) | copy-start | bytes 2359300
  42.4 1.9 %copy-start.2 = (bf16[64,2,24,512]{3,2,1,0:T(8,128)(2,1)S(1)}, bf16[64,2,24,512]{3,2,1,0:T(8,128)(2,1)}, u32[]{:S(2)}) copy-start(bf16[64,2,24,512]{3,2,1,0:T(8,128)(2,1)} %morph_ref.1) | copy-start | bytes 9437188
  44.3 0.7 copy-start.5
  56.7 23.5 %all-to-all-start.2 = ((bf16[16,6,8,512]{3,2,1,0:T(8,128)(2,1)}), bf16[16,6,8,512]{3,2,1,0:T(8,128)(2,1)S(1)}, u32[]{:S(2)}, u32[]{:S(2)}) async-start(bf16[16,6,8,512]{3,2,1,0:T(8,128)(2,1)} %get-tuple-element.14), calls=%async_computation.2 | async-start | bytes 1572864 | tf_op jit(solution)/shard_map/all_to_all | solution.py:255
  81.2 11.0 %all-to-all-start.3 = ((f32[32,1,128]{2,1,0:T(1,128)}), f32[32,1,128]{2,1,0:T(1,128)S(1)}, u32[]{:S(2)}, u32[]{:S(2)}) async-start(f32[32,1,128]{2,1,0:T(1,128)} %get-tuple-element.16), calls=%async_computation.3 | async-start | bytes 32768 | tf_op jit(solution)/shard_map/all_to_all | solution.py:315
